TPU v7x, 32 devices: a whole 2x2x4 slice. The times are simulated.
32 devices in a mesh: beam: 2 (over x), gx: 16 (over z, y, core).
Axes of the slice: x: 2, y: 2, z: 4, core: 2. Of those that a mesh axis runs over, the one named last changes fastest.
Arguments:
- filterbank: bfloat16 [4096, 2048], P(('beam', 'gx')), parts along dimension 0, may hold values from -61 to 61
- chan_delay: int32 [16, 2048], P(None, 'gx'), may hold values from 0 to 7
- sub_delay: int32 [1536, 64], replicated, may hold values from 0 to 15
- widths: int32 [1536], replicated, may hold values from 1 to 16
Outputs:
- snr: float32 [3072, 2048], P('beam', 'gx'), parts along dimension 0
There are 2 independent parts, one for each index of `beam`. A program takes and returns all parts, laid end to end along the dimension named above; an argument that names none is the same for every part. Nothing has to cross between parts.
All inputs are finite; a program needn't handle non-finite values.
Results may differ from a plain program's by a relative error of at most 0.00059.
Values may be sent and summed in bfloat16 or wider, within the bound.
No kernel may reach another device: no remote copies, remote signals or barrier semaphores. Data moves between devices by JAX's collectives and lax.ppermute only.
A program may use at most 128 MiB of HBM per device.

v0:
```python
import jax
import jax.numpy as jnp
from jax import lax
from jax.sharding import PartitionSpec as P

SUBCH = 32
DELAY_ONE = 8
DELAY_TWO = 16
WMAX = 16


def passed_along(block, axis, distance):
    devices = range(lax.axis_size(axis))
    route = [(i - distance, i) for i in devices if i - distance in devices]
    return lax.ppermute(block, axis, route)


def per_device(filterbank, chan_delay, sub_delay, widths):
    chan_count, samples = filterbank.shape
    groups = chan_delay.shape[0]
    device_count = lax.axis_size("gx")
    sub_count = chan_count // SUBCH
    slab_len = samples // device_count
    trials, band_count = sub_delay.shape
    per_group = trials // groups
    margin_len = DELAY_TWO + WMAX
    span_len = slab_len + WMAX
    padded = jnp.pad(filterbank, ((0, 0), (0, DELAY_ONE)))
    band_input = padded.reshape(sub_count, SUBCH, samples + DELAY_ONE)
    band_delays = jnp.transpose(chan_delay.reshape(groups, sub_count, SUBCH), (1, 0, 2))
    first_codes = jnp.arange(DELAY_ONE, dtype=jnp.int32)[None, :, None]

    def band_sum(inputs):
        band_rows, delay_rows = inputs
        stacked = jnp.stack(
            [band_rows[:, offset : offset + samples] for offset in range(DELAY_ONE)], 0
        )
        stacked = stacked.reshape(DELAY_ONE * SUBCH, samples)
        one_hot = (
            (delay_rows[:, None, :] == first_codes)
            .astype(jnp.bfloat16)
            .reshape(groups, DELAY_ONE * SUBCH)
        )
        return jnp.dot(one_hot, stacked, preferred_element_type=jnp.float32).astype(jnp.bfloat16)

    subbands = lax.map(band_sum, (band_input, band_delays))
    regrouped = lax.all_to_all(subbands, "gx", split_axis=2, concat_axis=0, tiled=True)
    following = passed_along(regrouped[:, :, :margin_len], "gx", -1)
    extended = jnp.concatenate([regrouped, following], 2)
    trial_delays = sub_delay.reshape(groups, per_group, band_count)
    second_codes = jnp.arange(DELAY_TWO, dtype=jnp.int32)[None, :, None]

    def group_series(inputs):
        group_index, delay_rows = inputs
        group_rows = lax.dynamic_index_in_dim(extended, group_index, 1, keepdims=False)
        stacked = jnp.stack(
            [group_rows[:, offset : offset + span_len] for offset in range(DELAY_TWO)], 0
        )
        stacked = stacked.reshape(DELAY_TWO * band_count, span_len)
        one_hot = (
            (delay_rows[:, None, :] == second_codes)
            .astype(jnp.bfloat16)
            .reshape(per_group, DELAY_TWO * band_count)
        )
        own_part = jnp.dot(one_hot, stacked[:, :slab_len], preferred_element_type=jnp.float32)
        tail_part = lax.dot_general(
            stacked[:, slab_len:],
            one_hot,
            (((0,), (1,)), ((), ())),
            preferred_element_type=jnp.float32,
        )
        return (own_part, tail_part)

    own_blocks, tail_blocks = lax.map(
        group_series, (jnp.arange(groups, dtype=jnp.int32), trial_delays)
    )
    own_series = own_blocks.reshape(trials, slab_len)
    tail_cols = jnp.transpose(tail_blocks, (0, 2, 1)).reshape(trials, WMAX)
    series = jnp.concatenate([own_series, tail_cols], 1)
    boxcar = jnp.zeros((trials, slab_len), jnp.float32)
    for offset in range(WMAX):
        boxcar = boxcar + jnp.where(
            offset < widths[:, None], series[:, offset : offset + slab_len], 0.0
        )
    totals, squares = lax.psum(
        (jnp.sum(own_series, axis=1), jnp.sum(own_series * own_series, axis=1)), "gx"
    )
    average = totals / samples
    variance = squares / samples - average * average
    width_float = widths.astype(jnp.float32)[:, None]
    return (boxcar - width_float * average[:, None]) / jnp.sqrt(
        width_float * (variance[:, None] + 1e-05)
    )


def solution(mesh):
    in_specs = (P(("beam", "gx"), None), P(None, "gx"), P(), P())
    out_specs = P("beam", "gx")
    return jax.shard_map(
        per_device, mesh=mesh, in_specs=in_specs, out_specs=out_specs, check_vma=False
    )
```

profile of v0, /device:TPU:0, one launch (start us, length us, event | category | flops | bytes accessed | tf_op | source)
XLA Modules:
  0.0 178.5 jit_solution(11185816409424602314)
XLA Ops:
  0.0 0.8 reshape.68
  0.8 1.1 pad.4
  1.9 4.6 %while.24 = (s32[]{:T(128)}, bf16[4,16,2048]{2,1,0:T(8,128)(2,1)S(1)}, s32[4,16,32]{2,0,1:T(4,128)S(1)}, bf16[4,32,2056]{2,1,0:T(8,128)(2,1)S(1)}, s32[]{:T(128)}) while((s32[]{:T(128)}, bf16[4,16,2048]{2,1,0:T(8,128)(2,1)S(1)}, s32[4,16,32]{2,0,1:T(4,128)S(1)}, bf16[4,32,2056]{2,1,0:T(8,128)(2,1)S(1)}, s32[]{:T(128)}) %tuple.66), condition=%wide.region_1.2_spmd.clone, body=%wide.region_0.1_spmd.clone.sunk | while | flops 16814080 | bytes 3486793 | solution.py:46
  2.7 0.3 fusion.95
  3.9 0.3 fusion.95
  5.0 0.3 fusion.95
  6.2 0.3 fusion.95
  6.5 1.4 copy.16
  7.8 2.1 %reshape.74 = bf16[16,2,4096]{2,1,0:T(2,128)(2,1)S(1)} reshape(bf16[2048,4,16]{2,1,0:T(4,128)(2,1)S(1)} %bitcast.225) | data formatting | bytes 524288
  10.0 17.2 %all_to_all.18 = bf16[16,2,4096]{2,1,0:T(2,128)(2,1)S(1)} all-to-all(bf16[16,2,4096]{2,1,0:T(2,128)(2,1)S(1)} %reshape.74), channel_id=1, replica_groups=mesh['beam'=2,'gx'=16] {'gx'}, dimensions={0} | all-to-all | bytes 524288 | tf_op jit(solution)/shard_map/all_to_all | solution.py:47
  27.2 1.4 reshape.75
  28.7 1.0 copy.17
  29.7 1.3 collective-permute-start
  31.2 1.9 %collective-permute-done = bf16[64,16,32]{2,0,1:T(8,128)(2,1)S(1)} collective-permute-done((bf16[64,16,32]{2,0,1:T(8,128)(2,1)S(1)}, bf16[64,16,32]{2,0,1:T(8,128)(2,1)S(1)}, u32[]{:S(2)}, u32[]{:S(2)}) %collective-permute-start) | collective-permute-done | bytes 65568 | tf_op jit(solution)/shard_map/ppermute | solution.py:15
  33.3 70.5 %while.25 = (s32[]{:T(128)}, f32[16,96,128]{2,1,0:T(8,128)S(1)}, f32[16,16,96]{2,1,0:T(8,128)S(1)}, s32[16,96,64]{1,0,2:T(8,128)S(1)}, s32[16]{0:T(128)S(1)}, /*...) while((s32[]{:T(128)}, f32[16,96,128]{2,1,0:T(8,128)S(1)}, ...), condition=%wide.region_3.4_spmd.clone, body=%wide.region_2.3_spmd.clone.sunk | while | flops 28409860 | bytes 2107547 | solution.py:74
  33.3 0.6 dynamic_slice.38
  37.1 0.3 fusion.100
  37.7 0.6 dynamic_slice.38
  41.5 0.3 fusion.100
  42.1 0.6 dynamic_slice.38
  45.9 0.3 fusion.100
  46.5 0.6 dynamic_slice.38
  50.3 0.3 fusion.100
  50.9 0.6 dynamic_slice.38
  54.7 0.3 fusion.100
  55.3 0.6 dynamic_slice.38
  59.2 0.3 fusion.100
  59.7 0.6 dynamic_slice.38
  63.6 0.3 fusion.100
  64.1 0.6 dynamic_slice.38
  68.0 0.3 fusion.100
  68.5 0.6 dynamic_slice.38
  72.4 0.3 fusion.100
  72.9 0.6 dynamic_slice.38
  76.8 0.3 fusion.100
  77.3 0.6 dynamic_slice.38
  81.7 0.6 dynamic_slice.38
  85.6 0.3 fusion.100
  86.1 0.6 dynamic_slice.38
  90.0 0.3 fusion.100
  90.5 0.6 dynamic_slice.38
  94.4 0.3 fusion.100
  94.9 0.6 dynamic_slice.38
  99.4 0.6 dynamic_slice.38
  103.2 0.3 fusion.100
  103.8 0.6 fusion.66
  104.8 61.7 %all-reduce.1 = (f32[1536]{0:T(1024)S(1)}, f32[1536]{0:T(1024)S(1)}) all-reduce(f32[1536]{0:T(1024)S(1)} %reduce_sum.25, f32[1536]{0:T(1024)S(1)} %reduce_sum.23), channel_id=1, replica_groups=mesh['beam'=2,'gx'=16] {'gx'}, use_global_device_ids=true, to_apply=%region_7.8 | all-reduce | flops 3072 | bytes 24576 | tf_op jit(solution)/shard_map/psum | solution.py:85
  166.5 11.9 %fusion.25 = f32[1536,128]{1,0:T(8,128)} fusion(f32[1536,128]{1,0:T(8,128)S(1)} %bitcast.229, f32[1536,16]{1,0:T(8,128)S(1)} %bitcast.228, f32[1536]{0:T(1024)S(1)} %get-tuple-element.146, f32[1536]{0:T(1024)S(1)} %get-tuple-element.145, pred[1536]{0:T(1024)(128)(4,1)S(1)} %get-tuple-element.162, pred[1536]{0:T(1024)(128)(4,1)S(1)} %get-tuple-element.148, ...), kind=kLoop, calls=%fused_computation.100 | loop fusion | flops 9437184 | bytes 1708032 | tf_op jit(solution)/shard_map/div | solution.py:91
  (409 shorter events, 32.7 us)
Async XLA Ops:
  27.2 3.8 %copy-start.1 = (s32[1536]{0:T(1024)S(1)}, s32[1536]{0:T(1024)}, u32[]{:S(2)}) copy-start(s32[1536]{0:T(1024)} %param.11) | copy-start | bytes 18436
  27.2 3.8 %copy-start = (s32[1536,64]{0,1:T(8,128)S(1)}, s32[1536,64]{0,1:T(8,128)}, u32[]{:S(2)}) copy-start(s32[1536,64]{0,1:T(8,128)} %param.10) | copy-start | bytes 1179652
  29.7 3.4 %collective-permute-start = (bf16[64,16,32]{2,0,1:T(8,128)(2,1)S(1)}, bf16[64,16,32]{2,0,1:T(8,128)(2,1)S(1)}, u32[]{:S(2)}, u32[]{:S(2)}) collective-permute-start(bf16[64,16,32]{2,0,1:T(8,128)(2,1)S(1)} %bitcast.231), channel_id=1, source_target_pairs={{1,0},{2,1},{3,2},{4,3},{5,4},{6,5},{7,6},{8,7},{9,8},{10,9},{11,1... | collective-permute-start | bytes 196616 | tf_op jit(solution)/shard_map/ppermute | solution.py:15
where the time goes:
time: 179 us; the launch traced here: 178 us
  blocking collectives  78.9 us (44%)
  local copies, waits for them, and re-layouts  42.3 us (24%)
  loops' own time  28.1 us (16%)
  other arithmetic  16 us (9%)
  matrix products  9.84 us (5%)
  waiting for transfers between devices  1.88 us (1%)
    psum x1, blocking collectives, per_device(): lax.psum((jnp.sum(own_series, axis=1), jnp.sum(own_series * own_series, a...  61.7 us
    another operation x1, loops' own time, per_device(): lax.map(group_series, (jnp.arange(groups, dtype=jnp.int32), trial_delays))  27.8 us
    while x268, local copies, waits for them, and re-layouts  20.8 us
    all_to_all x1, blocking collectives, per_device(): lax.all_to_all(subbands, 'gx', split_axis=2, concat_axis=0, tiled=True)  17.2 us
    div x1, other arithmetic, per_device(): (boxcar - width_float * average[:, None]) / jnp.sqrt(width_float * (varia...  11.9 us
    dynamic_slice x32, local copies, waits for them, and re-layouts, per_device(): lax.map(group_series, (jnp.arange(groups, dtype=jnp.int32), trial_delays))  9.85 us
    dot_general x16, matrix products, group_series(): jnp.dot(one_hot, stacked[:, :slab_len], preferred_element_type=jnp.float32)  5 us
  transfers between devices with their start and end apart: 1, of which 1 were waited for; matrix products, arithmetic and copies ran while one was open for 0% of the time, Pallas kernels for 0%

commit v1 on v0

v1 whole, which is shorter than its diff:
```python
import functools

import jax
import jax.numpy as jnp
from jax import lax
from jax.experimental import pallas as pl
from jax.experimental.pallas import tpu as pltpu
from jax.sharding import PartitionSpec as P

SUBCH = 32
DELAY_ONE = 8
DELAY_TWO = 16
WMAX = 16
LANES = 128
HALO = 32


def band_kernel(sub_count, groups, fb_ref, delay_ref, out_ref, rolled, tile):
    slabs = out_ref.shape[0]
    rows = sub_count * groups
    width = 2 * LANES
    chunks = slabs // 2
    delays = delay_ref[...]
    band_of = lax.broadcasted_iota(jnp.int32, delays.shape, 1) // SUBCH
    hot = []
    for offset in range(DELAY_ONE):
        for band in range(sub_count):
            hot.append(jnp.where((delays == offset) & (band_of == band), 1.0, 0.0))
    hot = jnp.concatenate(hot, 0).astype(jnp.bfloat16)
    lane = lax.broadcasted_iota(jnp.int32, (rows, width), 1)
    quarter = lax.broadcasted_iota(jnp.int32, (rows // 4, LANES), 1) // HALO
    out_ref[slabs - 1, rows:, :] = jnp.zeros((rows // 4, LANES), out_ref.dtype)
    rolled[lax.rem(chunks, 2)] = jnp.zeros(rolled.shape[1:], rolled.dtype)

    def body(i, carry):
        chunk = chunks - 1 - i
        now, later = lax.rem(chunk, 2), lax.rem(chunk + 1, 2)
        start = pl.multiple_of(chunk * width, width)
        parts = jnp.dot(hot, fb_ref[:, pl.ds(start, width)], preferred_element_type=jnp.float32)
        total = parts[:rows]
        for offset in range(1, DELAY_ONE):
            turned = pltpu.roll(parts[offset * rows : (offset + 1) * rows], width - offset, 1)
            following = jnp.concatenate([turned[:, :LANES], rolled[later, offset - 1]], 1)
            rolled[now, offset - 1] = turned[:, LANES:]
            total = total + jnp.where(lane < width - offset, turned, following)
        total = total.astype(jnp.bfloat16)
        for half in range(2):
            part = total[:, half * LANES : (half + 1) * LANES]
            slab = chunk * 2 + half
            out_ref[slab, :rows, :] = part
            tile[...] = part.astype(jnp.float32)
            packed = tile[pl.ds(0, rows // 4, 4), :]
            for q in range(1, 4):
                piece = pltpu.roll(tile[pl.ds(q, rows // 4, 4), :], HALO * q, 1)
                packed = jnp.where(quarter == q, piece, packed)
            packed = packed.astype(out_ref.dtype)
            if half:
                out_ref[slab - 1, rows:, :] = packed
            else:
                @pl.when(chunk > 0)
                def _():
                    out_ref[slab - 1, rows:, :] = packed
        return carry

    lax.fori_loop(0, chunks, body, 0)


def band_stage(filterbank, chan_delay, slabs):
    groups = chan_delay.shape[0]
    sub_count = filterbank.shape[0] // SUBCH
    rows = sub_count * groups
    return pl.pallas_call(
        functools.partial(band_kernel, sub_count, groups),
        out_shape=jax.ShapeDtypeStruct((slabs, rows + rows // 4, LANES), jnp.bfloat16),
        scratch_shapes=[
            pltpu.VMEM((2, DELAY_ONE - 1, rows, LANES), jnp.float32),
            pltpu.VMEM((rows, LANES), jnp.float32),
        ],
        name="bands",
    )(filterbank, chan_delay)


def trial_kernel(groups, per_group, held_ref, delay_ref, width_ref, box_ref, stat_ref, wide, slid, delays_at, series, stats):
    sources, row_count, _ = held_ref.shape
    bands, trials = delay_ref.shape
    per_source = bands // sources
    rows = per_source * groups
    blocks = trials // LANES
    copies = max(1, LANES // bands)
    span = LANES + WMAX
    base = 8
    rows = per_source * groups
    for block in range(blocks):
        delays_at[block] = delay_ref[:, block * LANES : (block + 1) * LANES]
    wide[...] = held_ref[...].reshape(sources * row_count, LANES).astype(jnp.float32)

    def turned(first_row, stride):
        picked = [
            wide[pl.ds(first_row + part * stride, sources, row_count), :] for part in range(per_source)
        ]
        return jnp.concatenate(picked * copies, 0).T

    def store(group, first, block):
        slid[group, base + first : base + first + block.shape[0], :] = block

    def store_slid(group, first, block):
        for copy in range(1, copies):
            low = copy * bands
            top = low + bands
            begin = base + first - copy
            slid[group, begin : begin + block.shape[0], low:top] = block[:, low:top]

    def spread(quad, carry):
        tails = turned(rows + quad, groups // 4)
        for q in range(4):
            group = quad * 4 + q
            body = turned(group, groups)
            tail = tails[q * HALO : (q + 1) * HALO]
            store(group, 0, body)
            store(group, LANES, tail)
            store_slid(group, 0, body)
            store_slid(group, LANES, tail)
        return carry

    lax.fori_loop(0, groups // 4, spread, 0)

    lane = lax.broadcasted_iota(jnp.int32, (span, LANES), 1)
    period = per_group // 32
    starts = [LANES * m // per_group for m in range(period)]
    splits = [per_group * (g + 1) - LANES * m for m, g in enumerate(starts)]

    def group_rows(group, offset):
        return slid[group, base + offset : base + offset + span, :]

    def cycle(turn, carry):
        for part in range(period):
            block = turn * period + part
            first_group = turn * (period * LANES // per_group) + starts[part]
            delays = jnp.concatenate(
                [delays_at[block, pl.ds(b, sources, per_source), :] for b in range(per_source)], 0
            )
            left = jnp.zeros((span, LANES), jnp.float32)
            right = jnp.zeros((span, LANES), jnp.float32)
            step = 2 * copies
            for offset in range(0, DELAY_TWO, step):
                hot = jnp.concatenate(
                    [jnp.where(delays == offset + e, 1.0, 0.0) for e in range(step)], 0
                )
                pieces = range(offset, offset + step, copies)
                left_rows = jnp.concatenate([group_rows(first_group, o) for o in pieces], 1)
                right_rows = jnp.concatenate([group_rows(first_group + 1, o) for o in pieces], 1)
                left = left + jnp.dot(left_rows, hot, preferred_element_type=jnp.float32)
                right = right + jnp.dot(right_rows, hot, preferred_element_type=jnp.float32)
            whole = jnp.where(lane < splits[part], left, right)
            series[...] = whole
            own = whole[:LANES]
            total = jnp.sum(own, 0, keepdims=True)
            centred = own - total * (1.0 / LANES)
            stats[pl.ds(block, 1), :] = total
            stats[pl.ds(blocks + block, 1), :] = jnp.sum(centred * centred, 0, keepdims=True)
            width = width_ref[pl.ds(block, 1), :]
            box = own
            for offset in range(1, WMAX):
                box = box + jnp.where(width > offset, series[offset : offset + LANES, :], 0.0)
            box_ref[block] = box
        return carry

    lax.fori_loop(0, blocks // period, cycle, 0)
    stat_ref[...] = jnp.broadcast_to(stats[...][None], stat_ref.shape)


def trial_stage(held, delays, widths, groups):
    sources, row_count, _ = held.shape
    bands, trials = delays.shape
    blocks = trials // LANES
    across = max(LANES, bands)
    return pl.pallas_call(
        functools.partial(trial_kernel, groups, trials // groups),
        out_shape=(
            jax.ShapeDtypeStruct((blocks, LANES, LANES), jnp.float32),
            jax.ShapeDtypeStruct((sources, 2 * blocks, LANES), jnp.float32),
        ),
        scratch_shapes=[
            pltpu.VMEM((sources * row_count, LANES), jnp.float32),
            pltpu.VMEM((groups, LANES + HALO + 8, across), jnp.float32),
            pltpu.VMEM((blocks, bands, LANES), jnp.int32),
            pltpu.VMEM((LANES + WMAX, LANES), jnp.float32),
            pltpu.VMEM((2 * blocks, LANES), jnp.float32),
        ],
        name="trials",
    )(held, delays, widths)


def snr_kernel(samples, box_ref, stat_ref, width_ref, out_ref):
    sources = stat_ref.shape[0]
    blocks = box_ref.shape[0]
    own = samples // sources
    totals = stat_ref[:, :blocks, :]
    average = jnp.sum(totals, 0) * (1.0 / samples)
    apart = totals * (1.0 / own) - average[None]
    squares = jnp.sum(stat_ref[:, blocks:, :], 0) + own * jnp.sum(apart * apart, 0)
    variance = squares * (1.0 / samples)
    width = width_ref[...].astype(jnp.float32)
    scale = 1.0 / jnp.sqrt(width * (variance + 1e-05))
    level = width * average
    for block in range(blocks):
        value = (box_ref[block] - level[block : block + 1]) * scale[block : block + 1]
        out_ref[block * LANES : (block + 1) * LANES, :] = value.T


def snr_stage(box, stats, widths, samples):
    blocks = box.shape[0]
    return pl.pallas_call(
        functools.partial(snr_kernel, samples),
        out_shape=jax.ShapeDtypeStruct((blocks * LANES, LANES), jnp.float32),
        name="snr",
    )(box, stats, widths)


def per_device(filterbank, chan_delay, sub_delay, widths):
    samples = filterbank.shape[1]
    groups = chan_delay.shape[0]
    slabs = lax.axis_size("gx")
    widths = widths.reshape(-1, LANES)
    sent = band_stage(filterbank, chan_delay, slabs)
    held = lax.all_to_all(sent, "gx", split_axis=0, concat_axis=0, tiled=True)
    box, stats = trial_stage(held, sub_delay.T, widths, groups)
    stats = lax.all_to_all(stats, "gx", split_axis=0, concat_axis=0, tiled=True)
    return snr_stage(box, stats, widths, samples)


def solution(mesh):
    in_specs = (P(("beam", "gx"), None), P(None, "gx"), P(), P())
    out_specs = P("beam", "gx")
    return jax.shard_map(
        per_device, mesh=mesh, in_specs=in_specs, out_specs=out_specs, check_vma=False
    )
```

time: 179 us -> 46.7 us (0.26)
  blocking collectives: 78.9 us -> 31.7 us
  local copies, waits for them, and re-layouts: 42.3 us -> 0 us
  loops' own time: 28.1 us -> 0 us
  other arithmetic: 16 us -> 0 us
  Pallas kernels: 0 us -> 14.7 us
  matrix products: 9.84 us -> 0 us
  waiting for transfers between devices: 1.88 us -> 0 us
    psum x1 -> x0, blocking collectives: 61.7 us -> none  [per_device(): lax.psum((jnp.sum(own_series, axis=1), jnp.sum(own_series * own_series, a...]
    another operation x2 -> x0, loops' own time: 28.1 us -> none  [the longest x1 27.8 us: per_device(): lax.map(group_series, (jnp.arange(groups, dtype=jnp.int32), trial_delays))]
    while x269 -> x0, local copies, waits for them, and re-layouts: 22.2 us -> none
    pallas_call x0 -> x3, Pallas kernels: none -> 14.7 us  [the longest x1 6.11 us: trial_stage(): pl.pallas_call(functools.partial(trial_kernel, groups, trials // groups),...]
    all_to_all x1 -> x2, blocking collectives: 17.2 us -> 31.7 us  [the longest x1 18.6 us: per_device(): held = lax.all_to_all(sent, 'gx', split_axis=0, concat_axis=0, tiled=True)]
    div x1 -> x0, other arithmetic: 11.9 us -> none  [per_device(): (boxcar - width_float * average[:, None]) / jnp.sqrt(width_float * (varia...]
    dynamic_slice x36 -> x0, local copies, waits for them, and re-layouts: 9.91 us -> none  [the longest x32 9.85 us: per_device(): lax.map(group_series, (jnp.arange(groups, dtype=jnp.int32), trial_delays))]
    dot_general x36 -> x0, matrix products: 9.84 us -> none  [the longest x16 5 us: group_series(): jnp.dot(one_hot, stacked[:, :slab_len], preferred_element_type=jnp.float32)]
  transfers between devices with their start and end apart: 1 -> 0, of which waited for: 1 -> 0; matrix products, arithmetic and copies ran while one was open for 0% -> 0% of each run, Pallas kernels for 0% -> 0%
where the time goes in v1:
time: 46.7 us; the launch traced here: 46.4 us
  blocking collectives  31.7 us (68%)
  Pallas kernels  14.7 us (31%)
    all_to_all x1, blocking collectives, per_device(): held = lax.all_to_all(sent, 'gx', split_axis=0, concat_axis=0, tiled=True)  18.6 us
    all_to_all x1, blocking collectives, per_device(): stats = lax.all_to_all(stats, 'gx', split_axis=0, concat_axis=0, tiled=True)  13.1 us
    pallas_call x1, Pallas kernels, trial_stage(): pl.pallas_call(functools.partial(trial_kernel, groups, trials // groups),...  6.11 us
    pallas_call x1, Pallas kernels, band_stage(): pl.pallas_call(functools.partial(band_kernel, sub_count, groups), out_sha...  6.09 us
    pallas_call x1, Pallas kernels, snr_stage(): pl.pallas_call(functools.partial(snr_kernel, samples), out_shape=jax.Shap...  2.45 us

profile of v1, /device:TPU:0, one launch (start us, length us, event | category | flops | bytes accessed | tf_op | source)
XLA Modules:
  0.0 46.4 jit_solution(5149902122370001036)
XLA Ops:
  0.0 6.1 %bands.1 = bf16[16,80,128]{2,1,0:T(8,128)(2,1)} custom-call(bf16[128,2048]{1,0:T(8,128)(2,1)} %fb_ref.1, s32[16,128]{1,0:T(8,128)} %delay_ref.1), custom_call_target="tpu_custom_call" | custom-call | tf_op jit(solution)/shard_map/bands/pallas_call | solution.py:72
  6.1 18.6 %all_to_all.10.held_ref = bf16[16,80,128]{2,1,0:T(8,128)(2,1)} all-to-all(bf16[16,80,128]{2,1,0:T(8,128)(2,1)} %bands.1), channel_id=1, replica_groups=mesh['beam'=2,'gx'=16] {'gx'}, dimensions={0} | all-to-all | bytes 655360 | tf_op jit(solution)/shard_map/all_to_all | solution.py:226
  24.7 6.1 %trials.1 = (f32[12,128,128]{2,1,0:T(8,128)}, f32[16,24,128]{2,1,0:T(8,128)}) custom-call(bf16[16,80,128]{2,1,0:T(8,128)(2,1)} %all_to_all.10.held_ref, s32[64,1536]{1,0:T(8,128)} %bitcast.2, s32[12,128]{1,0:T(8,128)} %bitcast.3), custom_call_target="tpu_custom_call" | custom-call | tf_op jit(solution)/shard_map/trials/pallas_call | solution.py:177
  30.8 13.1 %all_to_all.11.stat_ref = f32[16,24,128]{2,1,0:T(8,128)} all-to-all(f32[16,24,128]{2,1,0:T(8,128)} %get-tuple-element.8), channel_id=1, replica_groups=mesh['beam'=2,'gx'=16] {'gx'}, dimensions={0} | all-to-all | bytes 393216 | tf_op jit(solution)/shard_map/all_to_all | solution.py:228
  43.9 2.4 %snr.1 = f32[1536,128]{1,0:T(8,128)} custom-call(f32[12,128,128]{2,1,0:T(8,128)} %get-tuple-element.7.box_ref, f32[16,24,128]{2,1,0:T(8,128)} %all_to_all.11.stat_ref, s32[12,128]{1,0:T(8,128)} %bitcast.4), custom_call_target="tpu_custom_call" | custom-call | tf_op jit(solution)/shard_map/snr/pallas_call | solution.py:213

commit v2 on v1

--- a/solution.py
+++ b/solution.py
@@ -1,4 +1,5 @@
 import functools
+import math
 
 import jax
 import jax.numpy as jnp
@@ -13,71 +14,117 @@
 WMAX = 16
 LANES = 128
 HALO = 32
-
-
-def band_kernel(sub_count, groups, fb_ref, delay_ref, out_ref, rolled, tile):
+NEAR = 4
+
+
+def band_kernel(sub_count, groups, run, fb_hbm, delay_hbm, out_ref, held, delays_ref, carry, tile, sems):
     slabs = out_ref.shape[0]
+    channels, samples = fb_hbm.shape
     rows = sub_count * groups
-    width = 2 * LANES
-    chunks = slabs // 2
-    delays = delay_ref[...]
+    fetch_delays = pltpu.make_async_copy(delay_hbm, delays_ref, sems.at[0])
+    fetch = pltpu.make_async_copy(fb_hbm, held.at[:, :samples], sems.at[1])
+    fetch_delays.start()
+    fetch.start()
+    held[:, samples:] = jnp.zeros((channels, LANES), held.dtype)
+    carry[...] = jnp.zeros(carry.shape, carry.dtype)
+    out_ref[slabs - 1, rows:, :] = jnp.zeros((rows // 4, LANES), out_ref.dtype)
+    fetch_delays.wait()
+    delays = delays_ref[...]
     band_of = lax.broadcasted_iota(jnp.int32, delays.shape, 1) // SUBCH
     hot = []
-    for offset in range(DELAY_ONE):
+    for far in range(0, DELAY_ONE, NEAR):
         for band in range(sub_count):
-            hot.append(jnp.where((delays == offset) & (band_of == band), 1.0, 0.0))
+            hot.append(
+                jnp.concatenate(
+                    [
+                        jnp.where((delays == far + near) & (band_of == band), 1.0, 0.0)
+                        for near in range(NEAR)
+                    ],
+                    1,
+                )
+            )
     hot = jnp.concatenate(hot, 0).astype(jnp.bfloat16)
-    lane = lax.broadcasted_iota(jnp.int32, (rows, width), 1)
+    lane = lax.broadcasted_iota(jnp.int32, (channels, LANES), 1)
+    out_lane = lax.broadcasted_iota(jnp.int32, (rows, LANES), 1)
     quarter = lax.broadcasted_iota(jnp.int32, (rows // 4, LANES), 1) // HALO
-    out_ref[slabs - 1, rows:, :] = jnp.zeros((rows // 4, LANES), out_ref.dtype)
-    rolled[lax.rem(chunks, 2)] = jnp.zeros(rolled.shape[1:], rolled.dtype)
-
-    def body(i, carry):
-        chunk = chunks - 1 - i
-        now, later = lax.rem(chunk, 2), lax.rem(chunk + 1, 2)
-        start = pl.multiple_of(chunk * width, width)
-        parts = jnp.dot(hot, fb_ref[:, pl.ds(start, width)], preferred_element_type=jnp.float32)
-        total = parts[:rows]
-        for offset in range(1, DELAY_ONE):
-            turned = pltpu.roll(parts[offset * rows : (offset + 1) * rows], width - offset, 1)
-            following = jnp.concatenate([turned[:, :LANES], rolled[later, offset - 1]], 1)
-            rolled[now, offset - 1] = turned[:, LANES:]
-            total = total + jnp.where(lane < width - offset, turned, following)
-        total = total.astype(jnp.bfloat16)
-        for half in range(2):
-            part = total[:, half * LANES : (half + 1) * LANES]
-            slab = chunk * 2 + half
-            out_ref[slab, :rows, :] = part
-            tile[...] = part.astype(jnp.float32)
-            packed = tile[pl.ds(0, rows // 4, 4), :]
-            for q in range(1, 4):
-                piece = pltpu.roll(tile[pl.ds(q, rows // 4, 4), :], HALO * q, 1)
-                packed = jnp.where(quarter == q, piece, packed)
-            packed = packed.astype(out_ref.dtype)
-            if half:
-                out_ref[slab - 1, rows:, :] = packed
-            else:
-                @pl.when(chunk > 0)
-                def _():
+    fetch.wait()
+
+    def turn(i, _):
+        first = (slabs // run - 1 - i) * run
+
+        def tile_at(j):
+            return held[:, pl.ds(pl.multiple_of((first + j) * LANES, LANES), LANES)]
+
+        def turned_all(j):
+            block = tile_at(j)
+            return [block] + [pltpu.roll(block, LANES - near, 1) for near in range(1, NEAR)]
+
+        following = turned_all(run)
+        late = carry[...]
+        for pair in range(run // 2 - 1, -1, -1):
+            sides = [None, None]
+            for half in (1, 0):
+                here = turned_all(2 * pair + half)
+                sides[half] = jnp.concatenate(
+                    [here[0]]
+                    + [
+                        jnp.where(lane < LANES - near, here[near], following[near])
+                        for near in range(1, NEAR)
+                    ],
+                    0,
+                )
+                following = here
+            parts = jnp.dot(hot, jnp.concatenate(sides, 1), preferred_element_type=jnp.float32)
+            for half in (1, 0):
+                part = parts[:, half * LANES : (half + 1) * LANES]
+                total = part[:rows]
+                fresh = pltpu.roll(part[rows:], LANES - NEAR, 1)
+                total = total + jnp.where(out_lane < LANES - NEAR, fresh, late)
+                late = fresh
+                total = total.astype(jnp.bfloat16)
+                slot = 2 * pair + half
+                slab = first + slot
+                out_ref[slab, :rows, :] = total
+                tile[slot] = total.astype(jnp.float32)
+                packed = tile[slot, pl.ds(0, rows // 4, 4), :]
+                for q in range(1, 4):
+                    piece = pltpu.roll(tile[slot, pl.ds(q, rows // 4, 4), :], HALO * q, 1)
+                    packed = jnp.where(quarter == q, piece, packed)
+                packed = packed.astype(out_ref.dtype)
+                if slot:
                     out_ref[slab - 1, rows:, :] = packed
-        return carry
-
-    lax.fori_loop(0, chunks, body, 0)
+                else:
+                    @pl.when(slab > 0)
+                    def _():
+                        out_ref[slab - 1, rows:, :] = packed
+        carry[...] = late
+        return 0
+
+    if run == slabs:
+        turn(0, 0)
+    else:
+        lax.fori_loop(0, slabs // run, turn, 0)
 
 
 def band_stage(filterbank, chan_delay, slabs):
     groups = chan_delay.shape[0]
-    sub_count = filterbank.shape[0] // SUBCH
-    rows = sub_count * groups
+    channels, samples = filterbank.shape
+    rows = channels // SUBCH * groups
+    run = math.gcd(slabs, 16)
     return pl.pallas_call(
-        functools.partial(band_kernel, sub_count, groups),
+        functools.partial(band_kernel, channels // SUBCH, groups, run),
         out_shape=jax.ShapeDtypeStruct((slabs, rows + rows // 4, LANES), jnp.bfloat16),
+        in_specs=[pl.BlockSpec(memory_space=pltpu.HBM)] * 2,
         scratch_shapes=[
-            pltpu.VMEM((2, DELAY_ONE - 1, rows, LANES), jnp.float32),
+            pltpu.VMEM((channels, samples + LANES), jnp.bfloat16),
+            pltpu.VMEM(chan_delay.shape, jnp.int32),
             pltpu.VMEM((rows, LANES), jnp.float32),
+            pltpu.VMEM((run, rows, LANES), jnp.float32),
+            pltpu.SemaphoreType.DMA((2,)),
         ],
+        compiler_params=pltpu.CompilerParams(vmem_limit_bytes=(8 << 20) + 2 * filterbank.size),
         name="bands",
-    )(filterbank, chan_delay)
+    )(*(pltpu.with_memory_space_constraint(x, pltpu.HBM) for x in (filterbank, chan_delay)))
 
 
 def trial_kernel(groups, per_group, held_ref, delay_ref, width_ref, box_ref, stat_ref, wide, slid, delays_at, series, stats):
@@ -187,6 +234,7 @@
             pltpu.VMEM((LANES + WMAX, LANES), jnp.float32),
             pltpu.VMEM((2 * blocks, LANES), jnp.float32),
         ],
+        compiler_params=pltpu.CompilerParams(vmem_limit_bytes=(8 << 20) + 8 * DELAY_TWO * delays.size),
         name="trials",
     )(held, delays, widths)
 
@@ -213,6 +261,7 @@
     return pl.pallas_call(
         functools.partial(snr_kernel, samples),
         out_shape=jax.ShapeDtypeStruct((blocks * LANES, LANES), jnp.float32),
+        compiler_params=pltpu.CompilerParams(vmem_limit_bytes=8 << 20),
         name="snr",
     )(box, stats, widths)
 

time: 46.7 us -> 38.4 us (0.82)
  Pallas kernels: 14.7 us -> 7.78 us
  blocking collectives: 31.7 us -> 30.3 us
    pallas_call x1, Pallas kernels: 6.09 us -> 2.51 us  [band_stage(): pl.pallas_call(functools.partial(band_kernel, channels // SUBCH, groups,...]
    pallas_call x1, Pallas kernels: 6.11 us -> 4.07 us  [trial_stage(): pl.pallas_call(functools.partial(trial_kernel, groups, trials // groups),...]
    pallas_call x1, Pallas kernels: 2.45 us -> 1.2 us  [snr_stage(): pl.pallas_call(functools.partial(snr_kernel, samples), out_shape=jax.Shap...]
    all_to_all x1, blocking collectives: 13.1 us -> 11.9 us  [per_device(): stats = lax.all_to_all(stats, 'gx', split_axis=0, concat_axis=0, tiled=True)]
where the time goes in v2:
time: 38.4 us; the launch traced here: 38.1 us
  blocking collectives  30.3 us (79%)
  Pallas kernels  7.78 us (20%)
    all_to_all x1, blocking collectives, per_device(): held = lax.all_to_all(sent, 'gx', split_axis=0, concat_axis=0, tiled=True)  18.4 us
    all_to_all x1, blocking collectives, per_device(): stats = lax.all_to_all(stats, 'gx', split_axis=0, concat_axis=0, tiled=True)  11.9 us
    pallas_call x1, Pallas kernels, trial_stage(): pl.pallas_call(functools.partial(trial_kernel, groups, trials // groups),...  4.07 us
    pallas_call x1, Pallas kernels, band_stage(): pl.pallas_call(functools.partial(band_kernel, channels // SUBCH, groups,...  2.51 us
    pallas_call x1, Pallas kernels, snr_stage(): pl.pallas_call(functools.partial(snr_kernel, samples), out_shape=jax.Shap...  1.2 us

profile of v2, /device:TPU:0, one launch (start us, length us, event | category | flops | bytes accessed | tf_op | source)
XLA Modules:
  0.0 38.1 jit_solution(1323267960061066006)
XLA Ops:
  0.0 2.5 %bands.1 = bf16[16,80,128]{2,1,0:T(8,128)(2,1)S(1)} custom-call(bf16[128,2048]{1,0:T(8,128)(2,1)} %fb_hbm.1, s32[16,128]{1,0:T(8,128)} %delay_hbm.1), custom_call_target="tpu_custom_call" | custom-call | tf_op jit(solution)/shard_map/bands/pallas_call | solution.py:114
  2.5 0.0 copy-start
  2.5 0.0 copy-start.1
  2.5 18.4 %all_to_all.10.held_ref = bf16[16,80,128]{2,1,0:T(8,128)(2,1)S(1)} all-to-all(bf16[16,80,128]{2,1,0:T(8,128)(2,1)S(1)} %bands.1), channel_id=1, replica_groups=mesh['beam'=2,'gx'=16] {'gx'}, dimensions={0} | all-to-all | bytes 655360 | tf_op jit(solution)/shard_map/all_to_all | solution.py:275
  21.0 0.0 copy-done
  21.0 0.0 copy-done.1
  21.0 4.1 %trials.1 = (f32[12,128,128]{2,1,0:T(8,128)S(1)}, f32[16,24,128]{2,1,0:T(8,128)S(1)}) custom-call(bf16[16,80,128]{2,1,0:T(8,128)(2,1)S(1)} %all_to_all.10.held_ref, s32[64,1536]{1,0:T(8,128)S(1)} %bitcast.2, s32[12,128]{1,0:T(8,128)S(1)} %bitcast.3), custom_call_target="tpu_custom_call" | custom-call | tf_op jit(solution)/shard_map/trials/pallas_call | solution.py:224
  25.0 11.9 %all_to_all.11.stat_ref = f32[16,24,128]{2,1,0:T(8,128)S(1)} all-to-all(f32[16,24,128]{2,1,0:T(8,128)S(1)} %get-tuple-element.8), channel_id=1, replica_groups=mesh['beam'=2,'gx'=16] {'gx'}, dimensions={0} | all-to-all | bytes 393216 | tf_op jit(solution)/shard_map/all_to_all | solution.py:277
  36.9 1.2 %snr.1 = f32[1536,128]{1,0:T(8,128)} custom-call(f32[12,128,128]{2,1,0:T(8,128)S(1)} %get-tuple-element.7.box_ref, f32[16,24,128]{2,1,0:T(8,128)S(1)} %all_to_all.11.stat_ref, s32[12,128]{1,0:T(8,128)S(1)} %bitcast.4), custom_call_target="tpu_custom_call" | custom-call | tf_op jit(solution)/shard_map/snr/pallas_call | solution.py:261
Async XLA Ops:
  2.5 18.4 %copy-start = (s32[1536,64]{0,1:T(8,128)S(1)}, s32[1536,64]{0,1:T(8,128)}, u32[]{:S(2)}) copy-start(s32[1536,64]{0,1:T(8,128)} %param.6) | copy-start | bytes 1179652
  2.5 18.4 %copy-start.1 = (s32[1536]{0:T(1024)S(1)}, s32[1536]{0:T(1024)}, u32[]{:S(2)}) copy-start(s32[1536]{0:T(1024)} %param.7) | copy-start | bytes 18436

commit v3 on v2

--- a/solution.py
+++ b/solution.py
@@ -15,6 +15,7 @@
 LANES = 128
 HALO = 32
 NEAR = 4
+COST = pl.CostEstimate(flops=1 << 28, bytes_accessed=1 << 20, transcendentals=0)
 
 
 def band_kernel(sub_count, groups, run, fb_hbm, delay_hbm, out_ref, held, delays_ref, carry, tile, sems):
@@ -127,140 +128,217 @@
     )(*(pltpu.with_memory_space_constraint(x, pltpu.HBM) for x in (filterbank, chan_delay)))
 
 
-def trial_kernel(groups, per_group, held_ref, delay_ref, width_ref, box_ref, stat_ref, wide, slid, delays_at, series, stats):
+def group_lanes(row_pair, group, per_group):
+    start = group * per_group
+    first, shift = start // LANES, start % LANES
+    if not shift:
+        return row_pair(first)
+    front = pltpu.roll(row_pair(first), LANES - shift, 1)
+    if shift + per_group <= LANES:
+        return front
+    back = pltpu.roll(row_pair(first + 1), LANES - shift, 1)
+    lane = lax.broadcasted_iota(jnp.int32, front.shape, 1)
+    return jnp.where(lane < LANES - shift, front, back)
+
+
+def one_hot(delays, first, count):
+    return jnp.concatenate([jnp.where(delays == first + e, 1.0, 0.0) for e in range(count)], 0)
+
+
+def pieces_of(per_group):
+    period = per_group // HALO
+    starts = [LANES * m // per_group for m in range(period)]
+    splits = [per_group * (g + 1) - LANES * m for m, g in enumerate(starts)]
+    return period, starts, splits
+
+
+def series_kernel(whole, per_group, held_ref, delay_ref, series_ref, stat_ref, wide, slid, dense, near, rows_at):
     sources, row_count, _ = held_ref.shape
+    groups = series_ref.shape[0]
     bands, trials = delay_ref.shape
     per_source = bands // sources
     rows = per_source * groups
-    blocks = trials // LANES
+    pitch = row_count + 1
     copies = max(1, LANES // bands)
     span = LANES + WMAX
     base = 8
-    rows = per_source * groups
-    for block in range(blocks):
-        delays_at[block] = delay_ref[:, block * LANES : (block + 1) * LANES]
-    wide[...] = held_ref[...].reshape(sources * row_count, LANES).astype(jnp.float32)
+    for block in range(trials // LANES):
+        dense[block] = delay_ref[:, block * LANES : (block + 1) * LANES]
+
+    def ordered(block):
+        return jnp.concatenate(
+            [dense[block, pl.ds(b, sources, per_source), :] for b in range(per_source)], 0
+        )
+
+    for group in range(groups):
+        near[group] = group_lanes(ordered, group, per_group)
+    for source in range(sources):
+        wide[source * pitch : source * pitch + row_count, :] = held_ref[source].astype(jnp.float32)
 
     def turned(first_row, stride):
         picked = [
-            wide[pl.ds(first_row + part * stride, sources, row_count), :] for part in range(per_source)
+            wide[pl.ds(first_row + part * stride, sources, pitch), :] for part in range(per_source)
         ]
         return jnp.concatenate(picked * copies, 0).T
 
-    def store(group, first, block):
-        slid[group, base + first : base + first + block.shape[0], :] = block
-
-    def store_slid(group, first, block):
+    def store(q, first, block):
+        slid[q, base + first : base + first + block.shape[0], :] = block
+
+    def store_slid(q, first, block):
         for copy in range(1, copies):
             low = copy * bands
             top = low + bands
             begin = base + first - copy
-            slid[group, begin : begin + block.shape[0], low:top] = block[:, low:top]
-
-    def spread(quad, carry):
+            slid[q, begin : begin + block.shape[0], low:top] = block[:, low:top]
+
+    def quad_of(quad, at):
         tails = turned(rows + quad, groups // 4)
         for q in range(4):
             group = quad * 4 + q
+            place = at + q
             body = turned(group, groups)
             tail = tails[q * HALO : (q + 1) * HALO]
-            store(group, 0, body)
-            store(group, LANES, tail)
-            store_slid(group, 0, body)
-            store_slid(group, LANES, tail)
-        return carry
-
-    lax.fori_loop(0, groups // 4, spread, 0)
-
-    lane = lax.broadcasted_iota(jnp.int32, (span, LANES), 1)
-    period = per_group // 32
-    starts = [LANES * m // per_group for m in range(period)]
-    splits = [per_group * (g + 1) - LANES * m for m, g in enumerate(starts)]
-
-    def group_rows(group, offset):
-        return slid[group, base + offset : base + offset + span, :]
-
-    def cycle(turn, carry):
-        for part in range(period):
-            block = turn * period + part
-            first_group = turn * (period * LANES // per_group) + starts[part]
-            delays = jnp.concatenate(
-                [delays_at[block, pl.ds(b, sources, per_source), :] for b in range(per_source)], 0
-            )
-            left = jnp.zeros((span, LANES), jnp.float32)
-            right = jnp.zeros((span, LANES), jnp.float32)
+            store(place, 0, body)
+            store(place, LANES, tail)
+            store_slid(place, 0, body)
+            store_slid(place, LANES, tail)
+            out = jnp.zeros((span, LANES), jnp.float32)
             step = 2 * copies
             for offset in range(0, DELAY_TWO, step):
-                hot = jnp.concatenate(
-                    [jnp.where(delays == offset + e, 1.0, 0.0) for e in range(step)], 0
+                hot = one_hot(near[group], offset, step)
+                left = jnp.concatenate(
+                    [
+                        slid[place, base + o : base + o + span, :]
+                        for o in range(offset, offset + step, copies)
+                    ],
+                    1,
                 )
-                pieces = range(offset, offset + step, copies)
-                left_rows = jnp.concatenate([group_rows(first_group, o) for o in pieces], 1)
-                right_rows = jnp.concatenate([group_rows(first_group + 1, o) for o in pieces], 1)
-                left = left + jnp.dot(left_rows, hot, preferred_element_type=jnp.float32)
-                right = right + jnp.dot(right_rows, hot, preferred_element_type=jnp.float32)
-            whole = jnp.where(lane < splits[part], left, right)
-            series[...] = whole
-            own = whole[:LANES]
+                out = out + jnp.dot(left, hot, preferred_element_type=jnp.float32)
+            series_ref[group] = out
+            own = out[:LANES]
             total = jnp.sum(own, 0, keepdims=True)
             centred = own - total * (1.0 / LANES)
-            stats[pl.ds(block, 1), :] = total
-            stats[pl.ds(blocks + block, 1), :] = jnp.sum(centred * centred, 0, keepdims=True)
-            width = width_ref[pl.ds(block, 1), :]
-            box = own
-            for offset in range(1, WMAX):
-                box = box + jnp.where(width > offset, series[offset : offset + LANES, :], 0.0)
-            box_ref[block] = box
-        return carry
-
-    lax.fori_loop(0, blocks // period, cycle, 0)
-    stat_ref[...] = jnp.broadcast_to(stats[...][None], stat_ref.shape)
-
-
-def trial_stage(held, delays, widths, groups):
+            rows_at[0, pl.ds(group, 1), :] = total
+            rows_at[1, pl.ds(group, 1), :] = jnp.sum(centred * centred, 0, keepdims=True)
+
+    if whole:
+        for quad in range(groups // 4):
+            quad_of(quad, quad * 4)
+    else:
+
+        def turn(quad, _):
+            quad_of(quad, 0)
+            return 0
+
+        lax.fori_loop(0, groups // 4, turn, 0)
+
+    period, starts, splits = pieces_of(per_group)
+    cycle = period + 1
+    lane = lax.broadcasted_iota(jnp.int32, (groups // cycle, LANES), 1)
+    packed = []
+    for stat in range(2):
+        moved = [rows_at[stat, pl.ds(q, groups // cycle, cycle), :] for q in range(cycle)]
+        moved = [pltpu.roll(r, q * per_group % LANES, 1) if q else r for q, r in enumerate(moved)]
+        for start, split in zip(starts, splits):
+            packed.append(jnp.where(lane < split, moved[start], moved[start + 1]))
+    packed = jnp.concatenate(packed, 0)
+    stat_ref[...] = jnp.broadcast_to(packed[None], stat_ref.shape)
+
+
+def series_stage(held, delays, groups):
     sources, row_count, _ = held.shape
     bands, trials = delays.shape
-    blocks = trials // LANES
     across = max(LANES, bands)
+    whole = bands <= LANES
     return pl.pallas_call(
-        functools.partial(trial_kernel, groups, trials // groups),
+        functools.partial(series_kernel, whole, trials // groups),
         out_shape=(
-            jax.ShapeDtypeStruct((blocks, LANES, LANES), jnp.float32),
-            jax.ShapeDtypeStruct((sources, 2 * blocks, LANES), jnp.float32),
+            jax.ShapeDtypeStruct((groups, LANES + WMAX, LANES), jnp.float32),
+            jax.ShapeDtypeStruct((sources, 2 * trials // LANES, LANES), jnp.float32),
         ),
         scratch_shapes=[
-            pltpu.VMEM((sources * row_count, LANES), jnp.float32),
-            pltpu.VMEM((groups, LANES + HALO + 8, across), jnp.float32),
-            pltpu.VMEM((blocks, bands, LANES), jnp.int32),
-            pltpu.VMEM((LANES + WMAX, LANES), jnp.float32),
-            pltpu.VMEM((2 * blocks, LANES), jnp.float32),
+            pltpu.VMEM((sources * (row_count + 1) + 7, LANES), jnp.float32),
+            pltpu.VMEM((groups if whole else 4, LANES + HALO + 8, across), jnp.float32),
+            pltpu.VMEM((trials // LANES, bands, LANES), jnp.int32),
+            pltpu.VMEM((groups, bands, LANES), jnp.int32),
+            pltpu.VMEM((2, groups, LANES), jnp.float32),
         ],
-        compiler_params=pltpu.CompilerParams(vmem_limit_bytes=(8 << 20) + 8 * DELAY_TWO * delays.size),
-        name="trials",
-    )(held, delays, widths)
-
-
-def snr_kernel(samples, box_ref, stat_ref, width_ref, out_ref):
-    sources = stat_ref.shape[0]
-    blocks = box_ref.shape[0]
+        compiler_params=pltpu.CompilerParams(vmem_limit_bytes=(8 << 20) + (0 if whole else 32 << 20)),
+        name="series",
+    )(held, delays)
+
+
+def box_kernel(per_group, series_ref, width_ref, out_ref):
+    groups = series_ref.shape[0]
+    period, starts, splits = pieces_of(per_group)
+    cycle = period + 1
+    lane = lax.broadcasted_iota(jnp.int32, (LANES, LANES), 1)
+    for turn in range(groups // cycle):
+        moved = []
+        for q in range(cycle):
+            group = turn * cycle + q
+            width = group_lanes(lambda r: width_ref[r : r + 1, :], group, per_group)
+            box = series_ref[group, :LANES, :]
+            for offset in range(1, WMAX):
+                box = box + jnp.where(
+                    width > offset, series_ref[group, offset : offset + LANES, :], 0.0
+                )
+            moved.append(pltpu.roll(box, q * per_group % LANES, 1) if q else box)
+        for j, (start, split) in enumerate(zip(starts, splits)):
+            out_ref[turn * period + j] = jnp.where(lane < split, moved[start], moved[start + 1])
+
+
+def box_stage(series, widths, per_group):
+    blocks = widths.shape[0]
+    return pl.pallas_call(
+        functools.partial(box_kernel, per_group),
+        out_shape=jax.ShapeDtypeStruct((blocks, LANES, LANES), jnp.float32),
+        compiler_params=pltpu.CompilerParams(vmem_limit_bytes=8 << 20),
+        cost_estimate=COST,
+        name="box",
+    )(series, widths)
+
+
+def snr_kernel(samples, period, box_ref, stat_ref, width_ref, out_hbm, done, sems):
+    sources, stat_rows, _ = stat_ref.shape
+    blocks = stat_rows // 2
+    turns = blocks // period
     own = samples // sources
     totals = stat_ref[:, :blocks, :]
     average = jnp.sum(totals, 0) * (1.0 / samples)
     apart = totals * (1.0 / own) - average[None]
     squares = jnp.sum(stat_ref[:, blocks:, :], 0) + own * jnp.sum(apart * apart, 0)
     variance = squares * (1.0 / samples)
-    width = width_ref[...].astype(jnp.float32)
+    width = jnp.concatenate([width_ref[pl.ds(j, turns, period), :] for j in range(period)], 0)
+    width = width.astype(jnp.float32)
     scale = 1.0 / jnp.sqrt(width * (variance + 1e-05))
     level = width * average
-    for block in range(blocks):
-        value = (box_ref[block] - level[block : block + 1]) * scale[block : block + 1]
-        out_ref[block * LANES : (block + 1) * LANES, :] = value.T
-
-
-def snr_stage(box, stats, widths, samples):
-    blocks = box.shape[0]
+    copies = []
+    for turn in range(turns):
+        for j in range(period):
+            row = j * turns + turn
+            block = turn * period + j
+            value = (box_ref[block] - level[row : row + 1]) * scale[row : row + 1]
+            done[block * LANES : (block + 1) * LANES, :] = value.T
+        span = slice(turn * period * LANES, (turn + 1) * period * LANES)
+        copy = pltpu.make_async_copy(done.at[span, :], out_hbm.at[span, :], sems.at[turn])
+        copy.start()
+        copies.append(copy)
+    for copy in copies:
+        copy.wait()
+
+
+def snr_stage(box, stats, widths, samples, period):
+    blocks = widths.shape[0]
+    turns = blocks // period
     return pl.pallas_call(
-        functools.partial(snr_kernel, samples),
+        functools.partial(snr_kernel, samples, period),
         out_shape=jax.ShapeDtypeStruct((blocks * LANES, LANES), jnp.float32),
+        out_specs=pl.BlockSpec(memory_space=pltpu.HBM),
+        scratch_shapes=[
+            pltpu.VMEM((blocks * LANES, LANES), jnp.float32),
+            pltpu.SemaphoreType.DMA((turns,)),
+        ],
         compiler_params=pltpu.CompilerParams(vmem_limit_bytes=8 << 20),
         name="snr",
     )(box, stats, widths)
@@ -269,13 +347,15 @@
 def per_device(filterbank, chan_delay, sub_delay, widths):
     samples = filterbank.shape[1]
     groups = chan_delay.shape[0]
+    per_group = sub_delay.shape[0] // groups
     slabs = lax.axis_size("gx")
     widths = widths.reshape(-1, LANES)
     sent = band_stage(filterbank, chan_delay, slabs)
     held = lax.all_to_all(sent, "gx", split_axis=0, concat_axis=0, tiled=True)
-    box, stats = trial_stage(held, sub_delay.T, widths, groups)
+    series, stats = series_stage(held, sub_delay.T, groups)
+    box = box_stage(series, widths, per_group)
     stats = lax.all_to_all(stats, "gx", split_axis=0, concat_axis=0, tiled=True)
-    return snr_stage(box, stats, widths, samples)
+    return snr_stage(box, stats, widths, samples, pieces_of(per_group)[0])
 
 
 def solution(mesh):

time: 38.4 us -> 37.1 us (0.966)
  blocking collectives: 30.3 us -> 18.3 us
  waiting for transfers between devices: 0 us -> 7.51 us
  starting transfers between devices: 0 us -> 3.52 us
    all_to_all x1 -> x0, blocking collectives: 11.9 us -> none  [per_device(): stats = lax.all_to_all(stats, 'gx', split_axis=0, concat_axis=0, tiled=True)]
    all_to_all x0 -> x1, waiting for transfers between devices: none -> 7.51 us  [per_device(): stats = lax.all_to_all(stats, 'gx', split_axis=0, concat_axis=0, tiled=True)]
    all_to_all x0 -> x1, starting transfers between devices: none -> 3.52 us  [per_device(): stats = lax.all_to_all(stats, 'gx', split_axis=0, concat_axis=0, tiled=True)]
    pallas_call x2 -> x3, Pallas kernels: 5.27 us -> 4.89 us  [the longest x1 2.4 us: series_stage(): pl.pallas_call(functools.partial(series_kernel, whole, trials // groups),...]
  transfers between devices with their start and end apart: 0 -> 1, of which waited for: 0 -> 1; matrix products, arithmetic and copies ran while one was open for 0% -> 0% of each run, Pallas kernels for 0% -> 4%
where the time goes in v3:
time: 37.1 us; the launch traced here: 36.8 us
  blocking collectives  18.3 us (49%)
  waiting for transfers between devices  7.51 us (20%)
  Pallas kernels  7.45 us (20%)
  starting transfers between devices  3.52 us (9%)
    all_to_all x1, blocking collectives, per_device(): held = lax.all_to_all(sent, 'gx', split_axis=0, concat_axis=0, tiled=True)  18.3 us
    all_to_all x1, waiting for transfers between devices, per_device(): stats = lax.all_to_all(stats, 'gx', split_axis=0, concat_axis=0, tiled=True)  7.51 us
    all_to_all x1, starting transfers between devices, per_device(): stats = lax.all_to_all(stats, 'gx', split_axis=0, concat_axis=0, tiled=True)  3.52 us
    pallas_call x1, Pallas kernels, band_stage(): pl.pallas_call(functools.partial(band_kernel, channels // SUBCH, groups,...  2.56 us
    pallas_call x1, Pallas kernels, series_stage(): pl.pallas_call(functools.partial(series_kernel, whole, trials // groups),...  2.4 us
    pallas_call x1, Pallas kernels, box_stage(): pl.pallas_call(functools.partial(box_kernel, per_group), out_shape=jax.Sh...  1.4 us
    pallas_call x1, Pallas kernels, snr_stage(): pl.pallas_call(functools.partial(snr_kernel, samples, period), out_shape=...  1.09 us
  transfers between devices with their start and end apart: 1, of which 1 were waited for; matrix products, arithmetic and copies ran while one was open for 0% of the time, Pallas kernels for 4%

profile of v3, /device:TPU:0, one launch (start us, length us, event | category | flops | bytes accessed | tf_op | source)
XLA Modules:
  0.0 36.8 jit_solution(16370353236402014342)
XLA Ops:
  0.0 0.0 copy-start
  0.0 0.0 copy-start.1
  0.0 2.6 %bands.1 = bf16[16,80,128]{2,1,0:T(8,128)(2,1)S(1)} custom-call(bf16[128,2048]{1,0:T(8,128)(2,1)} %fb_hbm.1, s32[16,128]{1,0:T(8,128)} %delay_hbm.1), custom_call_target="tpu_custom_call" | custom-call | tf_op jit(solution)/shard_map/bands/pallas_call | solution.py:115
  2.6 18.3 %all_to_all.10.held_ref = bf16[16,80,128]{2,1,0:T(8,128)(2,1)S(1)} all-to-all(bf16[16,80,128]{2,1,0:T(8,128)(2,1)S(1)} %bands.1), channel_id=1, replica_groups=mesh['beam'=2,'gx'=16] {'gx'}, dimensions={0} | all-to-all | bytes 655360 | tf_op jit(solution)/shard_map/all_to_all | solution.py:354
  20.9 0.0 copy-done
  20.9 2.4 %series.1 = (f32[16,144,128]{2,1,0:T(8,128)S(1)}, f32[16,24,128]{2,1,0:T(8,128)}) custom-call(bf16[16,80,128]{2,1,0:T(8,128)(2,1)S(1)} %all_to_all.10.held_ref, s32[64,1536]{1,0:T(8,128)S(1)} %bitcast.2), custom_call_target="tpu_custom_call" | custom-call | tf_op jit(solution)/shard_map/series/pallas_call | solution.py:253
  23.3 3.5 %all-to-all-start.1 = ((f32[16,24,128]{2,1,0:T(8,128)}), f32[16,24,128]{2,1,0:T(8,128)S(1)}, u32[]{:S(2)}, u32[]{:S(2)}) async-start(f32[16,24,128]{2,1,0:T(8,128)} %get-tuple-element.8), calls=%async_computation.1 | async-start | bytes 393216 | tf_op jit(solution)/shard_map/all_to_all | solution.py:357
  26.8 0.0 copy-done.1
  26.8 1.4 %box.1.box_ref = f32[12,128,128]{2,1,0:T(8,128)S(1)} custom-call(f32[16,144,128]{2,1,0:T(8,128)S(1)} %get-tuple-element.7.series_ref, s32[12,128]{1,0:T(8,128)S(1)} %bitcast.3), custom_call_target="tpu_custom_call" | custom-call | flops 268435456 | bytes 1048576 | tf_op jit(solution)/shard_map/box/pallas_call | solution.py:293
  28.2 7.5 %all-to-all-done.1.stat_ref = f32[16,24,128]{2,1,0:T(8,128)S(1)} async-done(((f32[16,24,128]{2,1,0:T(8,128)}), f32[16,24,128]{2,1,0:T(8,128)S(1)}, u32[]{:S(2)}, u32[]{:S(2)}) %all-to-all-start.1) | async-done | bytes 196640 | tf_op jit(solution)/shard_map/all_to_all | solution.py:357
  35.7 1.1 %snr.1 = f32[1536,128]{1,0:T(8,128)} custom-call(f32[12,128,128]{2,1,0:T(8,128)S(1)} %box.1.box_ref, f32[16,24,128]{2,1,0:T(8,128)S(1)} %all-to-all-done.1.stat_ref, s32[12,128]{1,0:T(8,128)S(1)} %bitcast.4), custom_call_target="tpu_custom_call" | custom-call | tf_op jit(solution)/shard_map/snr/pallas_call | solution.py:334
Async XLA Ops:
  0.0 20.9 %copy-start = (s32[1536,64]{0,1:T(8,128)S(1)}, s32[1536,64]{0,1:T(8,128)}, u32[]{:S(2)}) copy-start(s32[1536,64]{0,1:T(8,128)} %param.6) | copy-start | bytes 1179652
  0.0 26.8 %copy-start.1 = (s32[1536]{0:T(1024)S(1)}, s32[1536]{0:T(1024)}, u32[]{:S(2)}) copy-start(s32[1536]{0:T(1024)} %param.7) | copy-start | bytes 18436
  23.3 12.5 %all-to-all-start.1 = ((f32[16,24,128]{2,1,0:T(8,128)}), f32[16,24,128]{2,1,0:T(8,128)S(1)}, u32[]{:S(2)}, u32[]{:S(2)}) async-start(f32[16,24,128]{2,1,0:T(8,128)} %get-tuple-element.8), calls=%async_computation.1 | async-start | bytes 393216 | tf_op jit(solution)/shard_map/all_to_all | solution.py:357

commit v4 on v3

--- a/solution.py
+++ b/solution.py
@@ -15,6 +15,9 @@
 LANES = 128
 HALO = 32
 NEAR = 4
+FAR = DELAY_TWO // 2
+FETCHES = 1
+PACE = 16
 COST = pl.CostEstimate(flops=1 << 28, bytes_accessed=1 << 20, transcendentals=0)
 
 
@@ -23,9 +26,18 @@
     channels, samples = fb_hbm.shape
     rows = sub_count * groups
     fetch_delays = pltpu.make_async_copy(delay_hbm, delays_ref, sems.at[0])
-    fetch = pltpu.make_async_copy(fb_hbm, held.at[:, :samples], sems.at[1])
+    piece = samples // FETCHES
+    fetches = [
+        pltpu.make_async_copy(
+            fb_hbm.at[:, p * piece : (p + 1) * piece],
+            held.at[:, p * piece : (p + 1) * piece],
+            sems.at[p + 1],
+        )
+        for p in range(FETCHES)
+    ]
     fetch_delays.start()
-    fetch.start()
+    for fetch in reversed(fetches):
+        fetch.start()
     held[:, samples:] = jnp.zeros((channels, LANES), held.dtype)
     carry[...] = jnp.zeros(carry.shape, carry.dtype)
     out_ref[slabs - 1, rows:, :] = jnp.zeros((rows // 4, LANES), out_ref.dtype)
@@ -47,8 +59,14 @@
     hot = jnp.concatenate(hot, 0).astype(jnp.bfloat16)
     lane = lax.broadcasted_iota(jnp.int32, (channels, LANES), 1)
     out_lane = lax.broadcasted_iota(jnp.int32, (rows, LANES), 1)
-    quarter = lax.broadcasted_iota(jnp.int32, (rows // 4, LANES), 1) // HALO
-    fetch.wait()
+    place = lax.broadcasted_iota(jnp.int32, (4 * LANES, LANES), 0)
+    place_out = lax.broadcasted_iota(jnp.int32, (4 * LANES, LANES), 1)
+    fold = (place % LANES < HALO) & (place // LANES * HALO + place % LANES == place_out)
+    fold = jnp.where(fold, 1.0, 0.0)
+    for fetch in fetches:
+        fetch.wait()
+
+    pace = math.gcd(run, PACE)
 
     def turn(i, _):
         first = (slabs // run - 1 - i) * run
@@ -62,11 +80,11 @@
 
         following = turned_all(run)
         late = carry[...]
-        for pair in range(run // 2 - 1, -1, -1):
-            sides = [None, None]
-            for half in (1, 0):
-                here = turned_all(2 * pair + half)
-                sides[half] = jnp.concatenate(
+        for pack in range(run // pace - 1, -1, -1):
+            sides = [None] * pace
+            for side in range(pace - 1, -1, -1):
+                here = turned_all(pace * pack + side)
+                sides[side] = jnp.concatenate(
                     [here[0]]
                     + [
                         jnp.where(lane < LANES - near, here[near], following[near])
@@ -76,28 +94,28 @@
                 )
                 following = here
             parts = jnp.dot(hot, jnp.concatenate(sides, 1), preferred_element_type=jnp.float32)
-            for half in (1, 0):
-                part = parts[:, half * LANES : (half + 1) * LANES]
+            for side in range(pace - 1, -1, -1):
+                part = parts[:, side * LANES : (side + 1) * LANES]
                 total = part[:rows]
                 fresh = pltpu.roll(part[rows:], LANES - NEAR, 1)
                 total = total + jnp.where(out_lane < LANES - NEAR, fresh, late)
                 late = fresh
                 total = total.astype(jnp.bfloat16)
-                slot = 2 * pair + half
-                slab = first + slot
-                out_ref[slab, :rows, :] = total
-                tile[slot] = total.astype(jnp.float32)
-                packed = tile[slot, pl.ds(0, rows // 4, 4), :]
-                for q in range(1, 4):
-                    piece = pltpu.roll(tile[slot, pl.ds(q, rows // 4, 4), :], HALO * q, 1)
-                    packed = jnp.where(quarter == q, piece, packed)
-                packed = packed.astype(out_ref.dtype)
-                if slot:
-                    out_ref[slab - 1, rows:, :] = packed
-                else:
-                    @pl.when(slab > 0)
-                    def _():
-                        out_ref[slab - 1, rows:, :] = packed
+                slot = pace * pack + side
+                out_ref[first + slot, :rows, :] = total
+                tile[slot * rows : (slot + 1) * rows, :] = total.astype(jnp.float32)
+        ends = jnp.concatenate(
+            [tile[pl.ds(q, run * rows // 4, 4), :] for q in range(4)], 1
+        )
+        ends = jnp.dot(ends, fold, preferred_element_type=jnp.float32).astype(out_ref.dtype)
+        for slot in range(run):
+            end = ends[slot * rows // 4 : (slot + 1) * rows // 4]
+            if slot:
+                out_ref[first + slot - 1, rows:, :] = end
+            else:
+                @pl.when(first > 0)
+                def _():
+                    out_ref[first - 1, rows:, :] = end
         carry[...] = late
         return 0
 
@@ -120,8 +138,8 @@
             pltpu.VMEM((channels, samples + LANES), jnp.bfloat16),
             pltpu.VMEM(chan_delay.shape, jnp.int32),
             pltpu.VMEM((rows, LANES), jnp.float32),
-            pltpu.VMEM((run, rows, LANES), jnp.float32),
-            pltpu.SemaphoreType.DMA((2,)),
+            pltpu.VMEM((run * rows, LANES), jnp.float32),
+            pltpu.SemaphoreType.DMA((FETCHES + 1,)),
         ],
         compiler_params=pltpu.CompilerParams(vmem_limit_bytes=(8 << 20) + 2 * filterbank.size),
         name="bands",
@@ -202,18 +220,21 @@
             store(place, LANES, tail)
             store_slid(place, 0, body)
             store_slid(place, LANES, tail)
-            out = jnp.zeros((span, LANES), jnp.float32)
+            both = jnp.zeros((span + FAR, 2 * LANES), jnp.float32)
             step = 2 * copies
-            for offset in range(0, DELAY_TWO, step):
-                hot = one_hot(near[group], offset, step)
+            for offset in range(0, FAR, step):
+                hot = jnp.concatenate(
+                    [one_hot(near[group], far + offset, step) for far in (0, FAR)], 1
+                )
                 left = jnp.concatenate(
                     [
-                        slid[place, base + o : base + o + span, :]
+                        slid[place, base + o : base + o + span + FAR, :]
                         for o in range(offset, offset + step, copies)
                     ],
                     1,
                 )
-                out = out + jnp.dot(left, hot, preferred_element_type=jnp.float32)
+                both = both + jnp.dot(left, hot, preferred_element_type=jnp.float32)
+            out = both[:span, :LANES] + both[FAR:, LANES:]
             series_ref[group] = out
             own = out[:LANES]
             total = jnp.sum(own, 0, keepdims=True)
@@ -241,8 +262,7 @@
         moved = [pltpu.roll(r, q * per_group % LANES, 1) if q else r for q, r in enumerate(moved)]
         for start, split in zip(starts, splits):
             packed.append(jnp.where(lane < split, moved[start], moved[start + 1]))
-    packed = jnp.concatenate(packed, 0)
-    stat_ref[...] = jnp.broadcast_to(packed[None], stat_ref.shape)
+    stat_ref[...] = jnp.concatenate(packed, 0)
 
 
 def series_stage(held, delays, groups):
@@ -254,7 +274,7 @@
         functools.partial(series_kernel, whole, trials // groups),
         out_shape=(
             jax.ShapeDtypeStruct((groups, LANES + WMAX, LANES), jnp.float32),
-            jax.ShapeDtypeStruct((sources, 2 * trials // LANES, LANES), jnp.float32),
+            jax.ShapeDtypeStruct((2 * trials // LANES, LANES), jnp.float32),
         ),
         scratch_shapes=[
             pltpu.VMEM((sources * (row_count + 1) + 7, LANES), jnp.float32),
@@ -268,21 +288,41 @@
     )(held, delays)
 
 
-def box_kernel(per_group, series_ref, width_ref, out_ref):
+def box_kernel(per_group, series_ref, width_ref, out_ref, pairs, ones, fours, threes):
     groups = series_ref.shape[0]
     period, starts, splits = pieces_of(per_group)
     cycle = period + 1
     lane = lax.broadcasted_iota(jnp.int32, (LANES, LANES), 1)
+
+    def window(ref, group, first, count):
+        return ref[group, first : first + count, :]
+
+    def boxes(group):
+        width = group_lanes(lambda r: width_ref[r : r + 1, :], group, per_group)
+        bits = [width & (1 << e) > 0 for e in range(5)]
+        top = LANES + 15
+        here = window(series_ref, group, 0, top)
+        pairs[group, :top, :] = here + window(series_ref, group, 1, top)
+        ones[group, :top, :] = jnp.where(bits[0], here, 0.0)
+        top = LANES + 12
+        two = window(pairs, group, 0, top)
+        fours[group, :top, :] = two + window(pairs, group, 2, top)
+        threes[group, :top, :] = jnp.where(
+            bits[1], two + window(ones, group, 2, top), window(ones, group, 0, top)
+        )
+        top = LANES + 8
+        four = window(fours, group, 0, top)
+        eight = four + window(fours, group, 4, top)
+        seven = jnp.where(
+            bits[2], four + window(threes, group, 4, top), window(threes, group, 0, top)
+        )
+        part = jnp.where(bits[3], eight[:LANES] + seven[8:], seven[:LANES])
+        return jnp.where(bits[4], eight[:LANES] + eight[8:], part)
+
     for turn in range(groups // cycle):
         moved = []
         for q in range(cycle):
-            group = turn * cycle + q
-            width = group_lanes(lambda r: width_ref[r : r + 1, :], group, per_group)
-            box = series_ref[group, :LANES, :]
-            for offset in range(1, WMAX):
-                box = box + jnp.where(
-                    width > offset, series_ref[group, offset : offset + LANES, :], 0.0
-                )
+            box = boxes(turn * cycle + q)
             moved.append(pltpu.roll(box, q * per_group % LANES, 1) if q else box)
         for j, (start, split) in enumerate(zip(starts, splits)):
             out_ref[turn * period + j] = jnp.where(lane < split, moved[start], moved[start + 1])
@@ -293,10 +333,29 @@
     return pl.pallas_call(
         functools.partial(box_kernel, per_group),
         out_shape=jax.ShapeDtypeStruct((blocks, LANES, LANES), jnp.float32),
-        compiler_params=pltpu.CompilerParams(vmem_limit_bytes=8 << 20),
+        scratch_shapes=[pltpu.VMEM(series.shape, jnp.float32)] * 4,
+        compiler_params=pltpu.CompilerParams(vmem_limit_bytes=12 << 20),
         cost_estimate=COST,
         name="box",
     )(series, widths)
+
+
+def pair_kernel(own_ref, other_ref, out_ref):
+    blocks = own_ref.shape[0] // 2
+    total = own_ref[:blocks] + other_ref[:blocks]
+    apart = own_ref[:blocks] - other_ref[:blocks]
+    squares = own_ref[blocks:] + other_ref[blocks:] + apart * apart * (0.5 / LANES)
+    both = jnp.concatenate([total, squares], 0)
+    out_ref[...] = jnp.broadcast_to(both[None], out_ref.shape)
+
+
+def pair_stage(own, other, peers):
+    return pl.pallas_call(
+        pair_kernel,
+        out_shape=jax.ShapeDtypeStruct((peers, *own.shape), jnp.float32),
+        compiler_params=pltpu.CompilerParams(vmem_limit_bytes=8 << 20),
+        name="pair",
+    )(own, other)
 
 
 def snr_kernel(samples, period, box_ref, stat_ref, width_ref, out_hbm, done, sems):
@@ -348,19 +407,27 @@
     samples = filterbank.shape[1]
     groups = chan_delay.shape[0]
     per_group = sub_delay.shape[0] // groups
-    slabs = lax.axis_size("gx")
+    chips, cores = lax.axis_size("chip"), lax.axis_size("core")
     widths = widths.reshape(-1, LANES)
-    sent = band_stage(filterbank, chan_delay, slabs)
-    held = lax.all_to_all(sent, "gx", split_axis=0, concat_axis=0, tiled=True)
+    sent = band_stage(filterbank, chan_delay, chips * cores)
+    held = lax.all_to_all(sent, ("chip", "core"), split_axis=0, concat_axis=0, tiled=True)
     series, stats = series_stage(held, sub_delay.T, groups)
+    other = lax.ppermute(stats, "core", [(0, 1), (1, 0)])
     box = box_stage(series, widths, per_group)
-    stats = lax.all_to_all(stats, "gx", split_axis=0, concat_axis=0, tiled=True)
+    other, box = lax.optimization_barrier((other, box))
+    stats = pair_stage(stats, other, chips)
+    stats = lax.all_to_all(stats, "chip", split_axis=0, concat_axis=0, tiled=True)
     return snr_stage(box, stats, widths, samples, pieces_of(per_group)[0])
 
 
 def solution(mesh):
-    in_specs = (P(("beam", "gx"), None), P(None, "gx"), P(), P())
-    out_specs = P("beam", "gx")
+    beams, devices = mesh.devices.shape
+    split = jax.sharding.Mesh(
+        mesh.devices.reshape(beams, devices // 2, 2), ("beam", "chip", "core")
+    )
+    lines = ("chip", "core")
+    in_specs = (P(("beam", *lines), None), P(None, lines), P(), P())
+    out_specs = P("beam", lines)
     return jax.shard_map(
-        per_device, mesh=mesh, in_specs=in_specs, out_specs=out_specs, check_vma=False
+        per_device, mesh=split, in_specs=in_specs, out_specs=out_specs, check_vma=False
     )

time: 37.1 us -> 34.2 us (0.922)
  blocking collectives: 18.3 us -> 28.4 us
  waiting for transfers between devices: 7.51 us -> 0.12 us
  starting transfers between devices: 3.52 us -> 0.12 us
  Pallas kernels: 7.45 us -> 5.32 us
    all_to_all x1 -> x2, blocking collectives: 18.3 us -> 28.4 us  [the longest x1 18.3 us: per_device(): lax.all_to_all(sent, ('chip', 'core'), split_axis=0, concat_axis=0, tiled...]
    all_to_all x1 -> x0, waiting for transfers between devices: 7.51 us -> none  [per_device(): stats = lax.all_to_all(stats, 'gx', split_axis=0, concat_axis=0, tiled=True)]
    all_to_all x1 -> x0, starting transfers between devices: 3.52 us -> none  [per_device(): stats = lax.all_to_all(stats, 'gx', split_axis=0, concat_axis=0, tiled=True)]
    pallas_call x1, Pallas kernels: 2.4 us -> 1.18 us  [series_stage(): pl.pallas_call(functools.partial(series_kernel, whole, trials // groups),...]
    pallas_call x1, Pallas kernels: 1.4 us -> 0.94 us  [box_stage(): pl.pallas_call(functools.partial(box_kernel, per_group), out_shape=jax.Sh...]
    pallas_call x1, Pallas kernels: 2.56 us -> 2.12 us  [band_stage(): pl.pallas_call(functools.partial(band_kernel, channels // SUBCH, groups,...]
  transfers between devices with their start and end apart: 1 -> 1, of which waited for: 1 -> 1; matrix products, arithmetic and copies ran while one was open for 0% -> 0% of each run, Pallas kernels for 4% -> 3%
where the time goes in v4:
time: 34.2 us; the launch traced here: 34 us
  blocking collectives  28.4 us (83%)
  Pallas kernels  5.32 us (16%)
    all_to_all x1, blocking collectives, per_device(): lax.all_to_all(sent, ('chip', 'core'), split_axis=0, concat_axis=0, tiled...  18.3 us
    all_to_all x1, blocking collectives, per_device(): lax.all_to_all(stats, 'chip', split_axis=0, concat_axis=0, tiled=True)  10.1 us
    pallas_call x1, Pallas kernels, band_stage(): pl.pallas_call(functools.partial(band_kernel, channels // SUBCH, groups,...  2.12 us
    pallas_call x1, Pallas kernels, series_stage(): pl.pallas_call(functools.partial(series_kernel, whole, trials // groups),...  1.18 us
    pallas_call x1, Pallas kernels, snr_stage(): pl.pallas_call(functools.partial(snr_kernel, samples, period), out_shape=...  1.08 us
    pallas_call x1, Pallas kernels, box_stage(): pl.pallas_call(functools.partial(box_kernel, per_group), out_shape=jax.Sh...  0.94 us
  transfers between devices with their start and end apart: 1, of which 1 were waited for; matrix products, arithmetic and copies ran while one was open for 0% of the time, Pallas kernels for 3%

profile of v4, /device:TPU:0, one launch (start us, length us, event | category | flops | bytes accessed | tf_op | source)
XLA Modules:
  0.0 34.0 jit_solution(8333852944298535757)
XLA Ops:
  0.0 0.0 copy-start
  0.0 0.0 copy-start.1
  0.0 2.1 %bands.1 = bf16[16,80,128]{2,1,0:T(8,128)(2,1)S(1)} custom-call(bf16[128,2048]{1,0:T(8,128)(2,1)} %fb_hbm.1, s32[16,128]{1,0:T(8,128)} %delay_hbm.1), custom_call_target="tpu_custom_call" | custom-call | tf_op jit(solution)/shard_map/bands/pallas_call | solution.py:133
  2.1 18.3 %all_to_all.10.held_ref = bf16[16,80,128]{2,1,0:T(8,128)(2,1)S(1)} all-to-all(bf16[16,80,128]{2,1,0:T(8,128)(2,1)S(1)} %bands.1), channel_id=1, replica_groups=mesh['beam'=2,'chip'=8,'core'=2] {'chip','core'}, dimensions={0} | all-to-all | bytes 655360 | tf_op jit(solution)/shard_map/all_to_all | solution.py:413
  20.4 0.0 copy-done
  20.4 1.2 %series.1 = (f32[16,144,128]{2,1,0:T(8,128)S(1)}, f32[24,128]{1,0:T(8,128)S(1)}) custom-call(bf16[16,80,128]{2,1,0:T(8,128)(2,1)S(1)} %all_to_all.10.held_ref, s32[64,1536]{1,0:T(8,128)S(1)} %bitcast.2), custom_call_target="tpu_custom_call" | custom-call | tf_op jit(solution)/shard_map/series/pallas_call | solution.py:273
  21.6 0.1 collective-permute-start
  21.7 0.0 copy-done.1
  21.7 0.9 %box.1.box_ref = f32[12,128,128]{2,1,0:T(8,128)S(1)} custom-call(f32[16,144,128]{2,1,0:T(8,128)S(1)} %get-tuple-element.10.series_ref, s32[12,128]{1,0:T(8,128)S(1)} %bitcast.3), custom_call_target="tpu_custom_call" | custom-call | flops 268435456 | bytes 1048576 | tf_op jit(solution)/shard_map/box/pallas_call | solution.py:333
  22.7 0.1 collective-permute-done.other_ref
  22.8 10.1 %all_to_all.11.stat_ref = f32[8,24,128]{2,1,0:T(8,128)S(1)} all-to-all(f32[8,24,128]{2,1,0:T(8,128)S(1)} %pair.1), channel_id=1, replica_groups=mesh['beam'=2,'chip'=8,'core'=2] {'chip'}, dimensions={0} | all-to-all | bytes 196608 | tf_op jit(solution)/shard_map/all_to_all | solution.py:419
  32.9 1.1 %snr.1 = f32[1536,128]{1,0:T(8,128)} custom-call(f32[12,128,128]{2,1,0:T(8,128)S(1)} %box.1.box_ref, f32[8,24,128]{2,1,0:T(8,128)S(1)} %all_to_all.11.stat_ref, s32[12,128]{1,0:T(8,128)S(1)} %bitcast.4), custom_call_target="tpu_custom_call" | custom-call | tf_op jit(solution)/shard_map/snr/pallas_call | solution.py:393
  (1 shorter events, 0.0 us)
Async XLA Ops:
  0.0 20.4 %copy-start = (s32[1536,64]{0,1:T(8,128)S(1)}, s32[1536,64]{0,1:T(8,128)}, u32[]{:S(2)}) copy-start(s32[1536,64]{0,1:T(8,128)} %param.6) | copy-start | bytes 1179652
  0.0 21.7 %copy-start.1 = (s32[1536]{0:T(1024)S(1)}, s32[1536]{0:T(1024)}, u32[]{:S(2)}) copy-start(s32[1536]{0:T(1024)} %param.7) | copy-start | bytes 18436
  21.6 1.2 %collective-permute-start = (f32[24,128]{1,0:T(8,128)S(1)}, f32[24,128]{1,0:T(8,128)S(1)}, u32[]{:S(2)}, u32[]{:S(2)}) collective-permute-start(f32[24,128]{1,0:T(8,128)S(1)} %get-tuple-element.9.own_ref), channel_id=1, source_target_pairs={{0,1},{1,0},{2,3},{3,2},{4,5},{5,4},{6,7},{7,6},{8,9},{9,8},{10,11... | collective-permute-start | bytes 36872 | tf_op jit(solution)/shard_map/ppermute | solution.py:415

commit v5 on v4

--- a/solution.py
+++ b/solution.py
@@ -17,6 +17,7 @@
 NEAR = 4
 FAR = DELAY_TWO // 2
 FETCHES = 1
+OUT_BLOCKS = 2
 PACE = 16
 COST = pl.CostEstimate(flops=1 << 28, bytes_accessed=1 << 20, transcendentals=0)
 
@@ -78,7 +79,7 @@
             block = tile_at(j)
             return [block] + [pltpu.roll(block, LANES - near, 1) for near in range(1, NEAR)]
 
-        following = turned_all(run)
+        following = [jnp.zeros((channels, LANES), held.dtype)] * NEAR if run == slabs else turned_all(run)
         late = carry[...]
         for pack in range(run // pace - 1, -1, -1):
             sides = [None] * pace
@@ -146,17 +147,14 @@
     )(*(pltpu.with_memory_space_constraint(x, pltpu.HBM) for x in (filterbank, chan_delay)))
 
 
-def group_lanes(row_pair, group, per_group):
+def group_lanes(block_rows, group, per_group):
     start = group * per_group
     first, shift = start // LANES, start % LANES
-    if not shift:
-        return row_pair(first)
-    front = pltpu.roll(row_pair(first), LANES - shift, 1)
+    front = block_rows(first)
     if shift + per_group <= LANES:
         return front
-    back = pltpu.roll(row_pair(first + 1), LANES - shift, 1)
     lane = lax.broadcasted_iota(jnp.int32, front.shape, 1)
-    return jnp.where(lane < LANES - shift, front, back)
+    return jnp.where(lane < shift, block_rows(first + 1), front)
 
 
 def one_hot(delays, first, count):
@@ -259,7 +257,6 @@
     packed = []
     for stat in range(2):
         moved = [rows_at[stat, pl.ds(q, groups // cycle, cycle), :] for q in range(cycle)]
-        moved = [pltpu.roll(r, q * per_group % LANES, 1) if q else r for q, r in enumerate(moved)]
         for start, split in zip(starts, splits):
             packed.append(jnp.where(lane < split, moved[start], moved[start + 1]))
     stat_ref[...] = jnp.concatenate(packed, 0)
@@ -320,10 +317,7 @@
         return jnp.where(bits[4], eight[:LANES] + eight[8:], part)
 
     for turn in range(groups // cycle):
-        moved = []
-        for q in range(cycle):
-            box = boxes(turn * cycle + q)
-            moved.append(pltpu.roll(box, q * per_group % LANES, 1) if q else box)
+        moved = [boxes(turn * cycle + q) for q in range(cycle)]
         for j, (start, split) in enumerate(zip(starts, splits)):
             out_ref[turn * period + j] = jnp.where(lane < split, moved[start], moved[start + 1])
 
@@ -370,33 +364,34 @@
     variance = squares * (1.0 / samples)
     width = jnp.concatenate([width_ref[pl.ds(j, turns, period), :] for j in range(period)], 0)
     width = width.astype(jnp.float32)
-    scale = 1.0 / jnp.sqrt(width * (variance + 1e-05))
+    scale = lax.rsqrt(width * (variance + 1e-05))
     level = width * average
     copies = []
-    for turn in range(turns):
-        for j in range(period):
-            row = j * turns + turn
-            block = turn * period + j
-            value = (box_ref[block] - level[row : row + 1]) * scale[row : row + 1]
-            done[block * LANES : (block + 1) * LANES, :] = value.T
-        span = slice(turn * period * LANES, (turn + 1) * period * LANES)
-        copy = pltpu.make_async_copy(done.at[span, :], out_hbm.at[span, :], sems.at[turn])
-        copy.start()
-        copies.append(copy)
+    for block in range(blocks):
+        row = block % period * turns + block // period
+        span = slice(block * LANES, (block + 1) * LANES)
+        value = (box_ref[block] - level[row : row + 1]) * scale[row : row + 1]
+        done[span, :] = value.T
+        if (block + 1) % OUT_BLOCKS == 0:
+            span = slice((block + 1 - OUT_BLOCKS) * LANES, (block + 1) * LANES)
+            copy = pltpu.make_async_copy(
+                done.at[span, :], out_hbm.at[span, :], sems.at[block // OUT_BLOCKS]
+            )
+            copy.start()
+            copies.append(copy)
     for copy in copies:
         copy.wait()
 
 
 def snr_stage(box, stats, widths, samples, period):
     blocks = widths.shape[0]
-    turns = blocks // period
     return pl.pallas_call(
         functools.partial(snr_kernel, samples, period),
         out_shape=jax.ShapeDtypeStruct((blocks * LANES, LANES), jnp.float32),
         out_specs=pl.BlockSpec(memory_space=pltpu.HBM),
         scratch_shapes=[
             pltpu.VMEM((blocks * LANES, LANES), jnp.float32),
-            pltpu.SemaphoreType.DMA((turns,)),
+            pltpu.SemaphoreType.DMA((blocks // OUT_BLOCKS,)),
         ],
         compiler_params=pltpu.CompilerParams(vmem_limit_bytes=8 << 20),
         name="snr",

time: 34.2 us -> 34 us (level)
  transfers between devices with their start and end apart: 1 -> 1, of which waited for: 1 -> 1; matrix products, arithmetic and copies ran while one was open for 0% -> 0% of each run, Pallas kernels for 3% -> 2%
where the time goes in v5:
time: 34 us; the launch traced here: 33.8 us
  blocking collectives  28.3 us (83%)
  Pallas kernels  5.09 us (15%)
    all_to_all x1, blocking collectives, per_device(): lax.all_to_all(sent, ('chip', 'core'), split_axis=0, concat_axis=0, tiled...  18.3 us
    all_to_all x1, blocking collectives, per_device(): lax.all_to_all(stats, 'chip', split_axis=0, concat_axis=0, tiled=True)  10 us
    pallas_call x1, Pallas kernels, band_stage(): pl.pallas_call(functools.partial(band_kernel, channels // SUBCH, groups,...  2.09 us
    pallas_call x1, Pallas kernels, series_stage(): pl.pallas_call(functools.partial(series_kernel, whole, trials // groups),...  1.09 us
    pallas_call x1, Pallas kernels, snr_stage(): pl.pallas_call(functools.partial(snr_kernel, samples, period), out_shape=...  1.05 us
    pallas_call x1, Pallas kernels, box_stage(): pl.pallas_call(functools.partial(box_kernel, per_group), out_shape=jax.Sh...  0.84 us
  transfers between devices with their start and end apart: 1, of which 1 were waited for; matrix products, arithmetic and copies ran while one was open for 0% of the time, Pallas kernels for 2%

profile of v5, /device:TPU:0, one launch (start us, length us, event | category | flops | bytes accessed | tf_op | source)
XLA Modules:
  0.0 33.8 jit_solution(7765140505266072937)
XLA Ops:
  0.0 0.0 copy-start
  0.0 0.0 copy-start.1
  0.0 2.1 %bands.1 = bf16[16,80,128]{2,1,0:T(8,128)(2,1)S(1)} custom-call(bf16[128,2048]{1,0:T(8,128)(2,1)} %fb_hbm.1, s32[16,128]{1,0:T(8,128)} %delay_hbm.1), custom_call_target="tpu_custom_call" | custom-call | tf_op jit(solution)/shard_map/bands/pallas_call | solution.py:134
  2.1 18.3 %all_to_all.10.held_ref = bf16[16,80,128]{2,1,0:T(8,128)(2,1)S(1)} all-to-all(bf16[16,80,128]{2,1,0:T(8,128)(2,1)S(1)} %bands.1), channel_id=1, replica_groups=mesh['beam'=2,'chip'=8,'core'=2] {'chip','core'}, dimensions={0} | all-to-all | bytes 655360 | tf_op jit(solution)/shard_map/all_to_all | solution.py:408
  20.4 0.0 copy-done
  20.4 1.1 %series.1 = (f32[16,144,128]{2,1,0:T(8,128)S(1)}, f32[24,128]{1,0:T(8,128)S(1)}) custom-call(bf16[16,80,128]{2,1,0:T(8,128)(2,1)S(1)} %all_to_all.10.held_ref, s32[64,1536]{1,0:T(8,128)S(1)} %bitcast.2), custom_call_target="tpu_custom_call" | custom-call | tf_op jit(solution)/shard_map/series/pallas_call | solution.py:270
  21.5 0.2 collective-permute-start
  21.6 0.0 copy-done.1
  21.7 0.8 %box.1.box_ref = f32[12,128,128]{2,1,0:T(8,128)S(1)} custom-call(f32[16,144,128]{2,1,0:T(8,128)S(1)} %get-tuple-element.10.series_ref, s32[12,128]{1,0:T(8,128)S(1)} %bitcast.3), custom_call_target="tpu_custom_call" | custom-call | flops 268435456 | bytes 1048576 | tf_op jit(solution)/shard_map/box/pallas_call | solution.py:327
  22.5 0.2 collective-permute-done.other_ref
  22.7 10.0 %all_to_all.11.stat_ref = f32[8,24,128]{2,1,0:T(8,128)S(1)} all-to-all(f32[8,24,128]{2,1,0:T(8,128)S(1)} %pair.1), channel_id=1, replica_groups=mesh['beam'=2,'chip'=8,'core'=2] {'chip'}, dimensions={0} | all-to-all | bytes 196608 | tf_op jit(solution)/shard_map/all_to_all | solution.py:414
  32.8 1.1 %snr.1 = f32[1536,128]{1,0:T(8,128)} custom-call(f32[12,128,128]{2,1,0:T(8,128)S(1)} %box.1.box_ref, f32[8,24,128]{2,1,0:T(8,128)S(1)} %all_to_all.11.stat_ref, s32[12,128]{1,0:T(8,128)S(1)} %bitcast.4), custom_call_target="tpu_custom_call" | custom-call | tf_op jit(solution)/shard_map/snr/pallas_call | solution.py:388
  (1 shorter events, 0.0 us)
Async XLA Ops:
  0.0 20.4 %copy-start = (s32[1536,64]{0,1:T(8,128)S(1)}, s32[1536,64]{0,1:T(8,128)}, u32[]{:S(2)}) copy-start(s32[1536,64]{0,1:T(8,128)} %param.6) | copy-start | bytes 1179652
  0.0 21.6 %copy-start.1 = (s32[1536]{0:T(1024)S(1)}, s32[1536]{0:T(1024)}, u32[]{:S(2)}) copy-start(s32[1536]{0:T(1024)} %param.7) | copy-start | bytes 18436
  21.5 1.2 %collective-permute-start = (f32[24,128]{1,0:T(8,128)S(1)}, f32[24,128]{1,0:T(8,128)S(1)}, u32[]{:S(2)}, u32[]{:S(2)}) collective-permute-start(f32[24,128]{1,0:T(8,128)S(1)} %get-tuple-element.9.own_ref), channel_id=1, source_target_pairs={{0,1},{1,0},{2,3},{3,2},{4,5},{5,4},{6,7},{7,6},{8,9},{9,8},{10,11... | collective-permute-start | bytes 36872 | tf_op jit(solution)/shard_map/ppermute | solution.py:410

commit v6 on v5

--- a/solution.py
+++ b/solution.py
@@ -41,22 +41,27 @@
         fetch.start()
     held[:, samples:] = jnp.zeros((channels, LANES), held.dtype)
     carry[...] = jnp.zeros(carry.shape, carry.dtype)
-    out_ref[slabs - 1, rows:, :] = jnp.zeros((rows // 4, LANES), out_ref.dtype)
+    part = rows // 2
+    for core in range(2):
+        out_ref[slabs - 2 + core, rows:, :] = jnp.zeros((rows // 8, LANES), out_ref.dtype)
     fetch_delays.wait()
     delays = delays_ref[...]
     band_of = lax.broadcasted_iota(jnp.int32, delays.shape, 1) // SUBCH
     hot = []
     for far in range(0, DELAY_ONE, NEAR):
-        for band in range(sub_count):
-            hot.append(
-                jnp.concatenate(
-                    [
-                        jnp.where((delays == far + near) & (band_of == band), 1.0, 0.0)
-                        for near in range(NEAR)
-                    ],
-                    1,
+        for core in range(2):
+            wanted = delays[core * groups // 2 : (core + 1) * groups // 2]
+            for band in range(sub_count):
+                mine = band_of[: groups // 2] == band
+                hot.append(
+                    jnp.concatenate(
+                        [
+                            jnp.where((wanted == far + near) & mine, 1.0, 0.0)
+                            for near in range(NEAR)
+                        ],
+                        1,
+                    )
                 )
-            )
     hot = jnp.concatenate(hot, 0).astype(jnp.bfloat16)
     lane = lax.broadcasted_iota(jnp.int32, (channels, LANES), 1)
     out_lane = lax.broadcasted_iota(jnp.int32, (rows, LANES), 1)
@@ -96,27 +101,34 @@
                 following = here
             parts = jnp.dot(hot, jnp.concatenate(sides, 1), preferred_element_type=jnp.float32)
             for side in range(pace - 1, -1, -1):
-                part = parts[:, side * LANES : (side + 1) * LANES]
-                total = part[:rows]
-                fresh = pltpu.roll(part[rows:], LANES - NEAR, 1)
+                here = parts[:, side * LANES : (side + 1) * LANES]
+                total = here[:rows]
+                fresh = pltpu.roll(here[rows:], LANES - NEAR, 1)
                 total = total + jnp.where(out_lane < LANES - NEAR, fresh, late)
                 late = fresh
                 total = total.astype(jnp.bfloat16)
                 slot = pace * pack + side
-                out_ref[first + slot, :rows, :] = total
-                tile[slot * rows : (slot + 1) * rows, :] = total.astype(jnp.float32)
+                lead = first + slot // 2 * 2
+                low = slot % 2 * part
+                for core in range(2):
+                    out_ref[lead + core, low : low + part, :] = total[core * part : (core + 1) * part]
+                if slot % 2 == 0:
+                    at = slot // 2 * rows
+                    tile[at : at + rows, :] = total.astype(jnp.float32)
         ends = jnp.concatenate(
-            [tile[pl.ds(q, run * rows // 4, 4), :] for q in range(4)], 1
+            [tile[pl.ds(q, run * rows // 8, 4), :] for q in range(4)], 1
         )
-        ends = jnp.dot(ends, fold, preferred_element_type=jnp.float32).astype(out_ref.dtype)
-        for slot in range(run):
-            end = ends[slot * rows // 4 : (slot + 1) * rows // 4]
-            if slot:
-                out_ref[first + slot - 1, rows:, :] = end
-            else:
-                @pl.when(first > 0)
-                def _():
-                    out_ref[first - 1, rows:, :] = end
+        ends = jnp.dot(ends, fold, preferred_element_type=jnp.float32)
+        for pair in range(run // 2):
+            for core in range(2):
+                at = (2 * pair + core) * rows // 8
+                end = ends[at : at + rows // 8].astype(out_ref.dtype)
+                if pair:
+                    out_ref[first + 2 * pair - 2 + core, rows:, :] = end
+                else:
+                    @pl.when(first > 0)
+                    def _():
+                        out_ref[first - 2 + core, rows:, :] = end
         carry[...] = late
         return 0
 
@@ -133,13 +145,13 @@
     run = math.gcd(slabs, 16)
     return pl.pallas_call(
         functools.partial(band_kernel, channels // SUBCH, groups, run),
-        out_shape=jax.ShapeDtypeStruct((slabs, rows + rows // 4, LANES), jnp.bfloat16),
+        out_shape=jax.ShapeDtypeStruct((slabs, rows + rows // 8, LANES), jnp.bfloat16),
         in_specs=[pl.BlockSpec(memory_space=pltpu.HBM)] * 2,
         scratch_shapes=[
             pltpu.VMEM((channels, samples + LANES), jnp.bfloat16),
             pltpu.VMEM(chan_delay.shape, jnp.int32),
             pltpu.VMEM((rows, LANES), jnp.float32),
-            pltpu.VMEM((run * rows, LANES), jnp.float32),
+            pltpu.VMEM((run * rows // 2, LANES), jnp.float32),
             pltpu.SemaphoreType.DMA((FETCHES + 1,)),
         ],
         compiler_params=pltpu.CompilerParams(vmem_limit_bytes=(8 << 20) + 2 * filterbank.size),
@@ -173,13 +185,17 @@
     groups = series_ref.shape[0]
     bands, trials = delay_ref.shape
     per_source = bands // sources
-    rows = per_source * groups
+    part = per_source * groups
+    blocks = trials // 2 // LANES
     pitch = row_count + 1
     copies = max(1, LANES // bands)
-    span = LANES + WMAX
+    slab = 2 * LANES
+    span = slab + WMAX
     base = 8
-    for block in range(trials // LANES):
-        dense[block] = delay_ref[:, block * LANES : (block + 1) * LANES]
+    lead = lax.axis_index("core") * blocks
+    for block in range(blocks):
+        at = pl.multiple_of((lead + block) * LANES, LANES)
+        dense[block] = delay_ref[:, pl.ds(at, LANES)]
 
     def ordered(block):
         return jnp.concatenate(
@@ -193,7 +209,7 @@
 
     def turned(first_row, stride):
         picked = [
-            wide[pl.ds(first_row + part * stride, sources, pitch), :] for part in range(per_source)
+            wide[pl.ds(first_row + b * stride, sources, pitch), :] for b in range(per_source)
         ]
         return jnp.concatenate(picked * copies, 0).T
 
@@ -208,16 +224,16 @@
             slid[q, begin : begin + block.shape[0], low:top] = block[:, low:top]
 
     def quad_of(quad, at):
-        tails = turned(rows + quad, groups // 4)
+        tails = turned(2 * part + quad, groups // 4)
         for q in range(4):
             group = quad * 4 + q
             place = at + q
-            body = turned(group, groups)
-            tail = tails[q * HALO : (q + 1) * HALO]
-            store(place, 0, body)
-            store(place, LANES, tail)
-            store_slid(place, 0, body)
-            store_slid(place, LANES, tail)
+            pieces = [turned(side * part + group, groups) for side in range(2)]
+            pieces.append(tails[q * HALO : (q + 1) * HALO])
+            for side, piece in enumerate(pieces):
+                store(place, side * LANES, piece)
+            for side, piece in enumerate(pieces):
+                store_slid(place, side * LANES, piece)
             both = jnp.zeros((span + FAR, 2 * LANES), jnp.float32)
             step = 2 * copies
             for offset in range(0, FAR, step):
@@ -234,9 +250,9 @@
                 both = both + jnp.dot(left, hot, preferred_element_type=jnp.float32)
             out = both[:span, :LANES] + both[FAR:, LANES:]
             series_ref[group] = out
-            own = out[:LANES]
+            own = out[:slab]
             total = jnp.sum(own, 0, keepdims=True)
-            centred = own - total * (1.0 / LANES)
+            centred = own - total * (1.0 / slab)
             rows_at[0, pl.ds(group, 1), :] = total
             rows_at[1, pl.ds(group, 1), :] = jnp.sum(centred * centred, 0, keepdims=True)
 
@@ -267,66 +283,82 @@
     bands, trials = delays.shape
     across = max(LANES, bands)
     whole = bands <= LANES
+    half = groups // 2
     return pl.pallas_call(
         functools.partial(series_kernel, whole, trials // groups),
         out_shape=(
-            jax.ShapeDtypeStruct((groups, LANES + WMAX, LANES), jnp.float32),
-            jax.ShapeDtypeStruct((2 * trials // LANES, LANES), jnp.float32),
+            jax.ShapeDtypeStruct((half, 2 * LANES + WMAX, LANES), jnp.float32),
+            jax.ShapeDtypeStruct((trials // LANES, LANES), jnp.float32),
         ),
         scratch_shapes=[
             pltpu.VMEM((sources * (row_count + 1) + 7, LANES), jnp.float32),
-            pltpu.VMEM((groups if whole else 4, LANES + HALO + 8, across), jnp.float32),
-            pltpu.VMEM((trials // LANES, bands, LANES), jnp.int32),
-            pltpu.VMEM((groups, bands, LANES), jnp.int32),
-            pltpu.VMEM((2, groups, LANES), jnp.float32),
+            pltpu.VMEM((half if whole else 4, 2 * LANES + HALO + 8, across), jnp.float32),
+            pltpu.VMEM((trials // 2 // LANES, bands, LANES), jnp.int32),
+            pltpu.VMEM((half, bands, LANES), jnp.int32),
+            pltpu.VMEM((2, half, LANES), jnp.float32),
         ],
         compiler_params=pltpu.CompilerParams(vmem_limit_bytes=(8 << 20) + (0 if whole else 32 << 20)),
         name="series",
     )(held, delays)
 
 
-def box_kernel(per_group, series_ref, width_ref, out_ref, pairs, ones, fours, threes):
+def box_kernel(per_group, series_ref, width_ref, keep_ref, send_ref, pairs, ones, fours, threes):
     groups = series_ref.shape[0]
+    slab = 2 * LANES
     period, starts, splits = pieces_of(per_group)
     cycle = period + 1
+    blocks = keep_ref.shape[0]
+    core = lax.axis_index("core")
     lane = lax.broadcasted_iota(jnp.int32, (LANES, LANES), 1)
 
     def window(ref, group, first, count):
         return ref[group, first : first + count, :]
 
     def boxes(group):
-        width = group_lanes(lambda r: width_ref[r : r + 1, :], group, per_group)
+        width = group_lanes(
+            lambda r: width_ref[pl.ds(core * blocks + r, 1), :], group, per_group
+        )
         bits = [width & (1 << e) > 0 for e in range(5)]
-        top = LANES + 15
+        top = slab + 15
         here = window(series_ref, group, 0, top)
         pairs[group, :top, :] = here + window(series_ref, group, 1, top)
         ones[group, :top, :] = jnp.where(bits[0], here, 0.0)
-        top = LANES + 12
+        top = slab + 12
         two = window(pairs, group, 0, top)
         fours[group, :top, :] = two + window(pairs, group, 2, top)
         threes[group, :top, :] = jnp.where(
             bits[1], two + window(ones, group, 2, top), window(ones, group, 0, top)
         )
-        top = LANES + 8
-        four = window(fours, group, 0, top)
-        eight = four + window(fours, group, 4, top)
-        seven = jnp.where(
-            bits[2], four + window(threes, group, 4, top), window(threes, group, 0, top)
-        )
-        part = jnp.where(bits[3], eight[:LANES] + seven[8:], seven[:LANES])
-        return jnp.where(bits[4], eight[:LANES] + eight[8:], part)
+        sides = []
+        for side in range(0, slab, LANES):
+            top = LANES + 8
+            four = window(fours, group, side, top)
+            eight = four + window(fours, group, side + 4, top)
+            seven = jnp.where(
+                bits[2],
+                four + window(threes, group, side + 4, top),
+                window(threes, group, side, top),
+            )
+            some = jnp.where(bits[3], eight[:LANES] + seven[8:], seven[:LANES])
+            sides.append(jnp.where(bits[4], eight[:LANES] + eight[8:], some))
+        return sides
 
     for turn in range(groups // cycle):
         moved = [boxes(turn * cycle + q) for q in range(cycle)]
         for j, (start, split) in enumerate(zip(starts, splits)):
-            out_ref[turn * period + j] = jnp.where(lane < split, moved[start], moved[start + 1])
+            early, late = (
+                jnp.where(lane < split, moved[start][side], moved[start + 1][side])
+                for side in range(2)
+            )
+            keep_ref[turn * period + j] = jnp.where(core == 0, early, late)
+            send_ref[turn * period + j] = jnp.where(core == 0, late, early)
 
 
 def box_stage(series, widths, per_group):
-    blocks = widths.shape[0]
+    blocks = widths.shape[0] // 2
     return pl.pallas_call(
         functools.partial(box_kernel, per_group),
-        out_shape=jax.ShapeDtypeStruct((blocks, LANES, LANES), jnp.float32),
+        out_shape=[jax.ShapeDtypeStruct((blocks, LANES, LANES), jnp.float32)] * 2,
         scratch_shapes=[pltpu.VMEM(series.shape, jnp.float32)] * 4,
         compiler_params=pltpu.CompilerParams(vmem_limit_bytes=12 << 20),
         cost_estimate=COST,
@@ -335,55 +367,65 @@
 
 
 def pair_kernel(own_ref, other_ref, out_ref):
-    blocks = own_ref.shape[0] // 2
-    total = own_ref[:blocks] + other_ref[:blocks]
-    apart = own_ref[:blocks] - other_ref[:blocks]
-    squares = own_ref[blocks:] + other_ref[blocks:] + apart * apart * (0.5 / LANES)
-    both = jnp.concatenate([total, squares], 0)
+    half = own_ref.shape[0] // 2
+    own, other = own_ref[...], other_ref[...]
+    first = lax.axis_index("core") == 0
+    low = jnp.where(first, own, other)
+    high = jnp.where(first, other, own)
+    both = jnp.concatenate([low[:half], high[:half], low[half:], high[half:]], 0)
     out_ref[...] = jnp.broadcast_to(both[None], out_ref.shape)
 
 
 def pair_stage(own, other, peers):
     return pl.pallas_call(
         pair_kernel,
-        out_shape=jax.ShapeDtypeStruct((peers, *own.shape), jnp.float32),
+        out_shape=jax.ShapeDtypeStruct((peers, 2 * own.shape[0], LANES), jnp.float32),
         compiler_params=pltpu.CompilerParams(vmem_limit_bytes=8 << 20),
         name="pair",
     )(own, other)
 
 
-def snr_kernel(samples, period, box_ref, stat_ref, width_ref, out_hbm, done, sems):
+def snr_kernel(samples, period, keep_ref, came_ref, stat_ref, width_ref, out_hbm, done, levels, sems):
     sources, stat_rows, _ = stat_ref.shape
     blocks = stat_rows // 2
-    turns = blocks // period
+    half = blocks // 2
+    turns = half // period
     own = samples // sources
     totals = stat_ref[:, :blocks, :]
     average = jnp.sum(totals, 0) * (1.0 / samples)
     apart = totals * (1.0 / own) - average[None]
     squares = jnp.sum(stat_ref[:, blocks:, :], 0) + own * jnp.sum(apart * apart, 0)
     variance = squares * (1.0 / samples)
-    width = jnp.concatenate([width_ref[pl.ds(j, turns, period), :] for j in range(period)], 0)
+    width = jnp.concatenate(
+        [width_ref[pl.ds(c * half + j, turns, period), :] for c in range(2) for j in range(period)], 0
+    )
     width = width.astype(jnp.float32)
-    scale = lax.rsqrt(width * (variance + 1e-05))
-    level = width * average
+    levels[0] = width * average
+    levels[1] = lax.rsqrt(width * (variance + 1e-05))
+    core = lax.axis_index("core")
     copies = []
-    for block in range(blocks):
-        row = block % period * turns + block // period
-        span = slice(block * LANES, (block + 1) * LANES)
-        value = (box_ref[block] - level[row : row + 1]) * scale[row : row + 1]
-        done[span, :] = value.T
-        if (block + 1) % OUT_BLOCKS == 0:
-            span = slice((block + 1 - OUT_BLOCKS) * LANES, (block + 1) * LANES)
-            copy = pltpu.make_async_copy(
-                done.at[span, :], out_hbm.at[span, :], sems.at[block // OUT_BLOCKS]
-            )
-            copy.start()
-            copies.append(copy)
+    for order, (box_ref, place) in enumerate(((keep_ref, core), (came_ref, 1 - core))):
+        for block in range(half):
+            row = place * half + block % period * turns + block // period
+            at = order * half + block
+            level = levels[0, pl.ds(row, 1), :]
+            scale = levels[1, pl.ds(row, 1), :]
+            done[at * LANES : (at + 1) * LANES, :] = ((box_ref[block] - level) * scale).T
+            if (block + 1) % OUT_BLOCKS == 0:
+                size = OUT_BLOCKS * LANES
+                target = pl.multiple_of((place * half + block + 1 - OUT_BLOCKS) * LANES, LANES)
+                copy = pltpu.make_async_copy(
+                    done.at[(at + 1) * LANES - size : (at + 1) * LANES, :],
+                    out_hbm.at[pl.ds(target, size), :],
+                    sems.at[at // OUT_BLOCKS],
+                )
+                copy.start()
+                copies.append(copy)
     for copy in copies:
         copy.wait()
 
 
-def snr_stage(box, stats, widths, samples, period):
+def snr_stage(keep, came, stats, widths, samples, period):
     blocks = widths.shape[0]
     return pl.pallas_call(
         functools.partial(snr_kernel, samples, period),
@@ -391,11 +433,12 @@
         out_specs=pl.BlockSpec(memory_space=pltpu.HBM),
         scratch_shapes=[
             pltpu.VMEM((blocks * LANES, LANES), jnp.float32),
+            pltpu.VMEM((2, blocks, LANES), jnp.float32),
             pltpu.SemaphoreType.DMA((blocks // OUT_BLOCKS,)),
         ],
         compiler_params=pltpu.CompilerParams(vmem_limit_bytes=8 << 20),
         name="snr",
-    )(box, stats, widths)
+    )(keep, came, stats, widths)
 
 
 def per_device(filterbank, chan_delay, sub_delay, widths):
@@ -407,12 +450,14 @@
     sent = band_stage(filterbank, chan_delay, chips * cores)
     held = lax.all_to_all(sent, ("chip", "core"), split_axis=0, concat_axis=0, tiled=True)
     series, stats = series_stage(held, sub_delay.T, groups)
-    other = lax.ppermute(stats, "core", [(0, 1), (1, 0)])
-    box = box_stage(series, widths, per_group)
-    other, box = lax.optimization_barrier((other, box))
+    swap = [(0, 1), (1, 0)]
+    other = lax.ppermute(stats, "core", swap)
+    keep, send = box_stage(series, widths, per_group)
+    other, send = lax.optimization_barrier((other, send))
+    came = lax.ppermute(send, "core", swap)
     stats = pair_stage(stats, other, chips)
     stats = lax.all_to_all(stats, "chip", split_axis=0, concat_axis=0, tiled=True)
-    return snr_stage(box, stats, widths, samples, pieces_of(per_group)[0])
+    return snr_stage(keep, came, stats, widths, samples, pieces_of(per_group)[0])
 
 
 def solution(mesh):

time: 34 us -> 33.6 us (0.988)
  blocking collectives: 28.3 us -> 27.6 us
  starting transfers between devices: 0.17 us -> 0.54 us
    all_to_all x1, blocking collectives: 18.3 us -> 17.8 us  [per_device(): lax.all_to_all(sent, ('chip', 'core'), split_axis=0, concat_axis=0, tiled...]
    ppermute x1 -> x2, starting transfers between devices: 0.17 us -> 0.54 us  [the longest x1 0.36 us: per_device(): came = lax.ppermute(send, 'core', swap)]
  transfers between devices with their start and end apart: 1 -> 2, of which waited for: 1 -> 1; matrix products, arithmetic and copies ran while one was open for 0% -> 0% of each run, Pallas kernels for 2% -> 3%
where the time goes in v6:
time: 33.6 us; the launch traced here: 33.4 us
  blocking collectives  27.6 us (82%)
  Pallas kernels  5.11 us (15%)
  starting transfers between devices  0.54 us (2%)
    all_to_all x1, blocking collectives, per_device(): lax.all_to_all(sent, ('chip', 'core'), split_axis=0, concat_axis=0, tiled...  17.8 us
    all_to_all x1, blocking collectives, per_device(): lax.all_to_all(stats, 'chip', split_axis=0, concat_axis=0, tiled=True)  9.83 us
    pallas_call x1, Pallas kernels, band_stage(): pl.pallas_call(functools.partial(band_kernel, channels // SUBCH, groups,...  2.09 us
    pallas_call x1, Pallas kernels, snr_stage(): pl.pallas_call(functools.partial(snr_kernel, samples, period), out_shape=...  1.1 us
    pallas_call x1, Pallas kernels, series_stage(): pl.pallas_call(functools.partial(series_kernel, whole, trials // groups),...  0.97 us
    pallas_call x1, Pallas kernels, box_stage(): pl.pallas_call(functools.partial(box_kernel, per_group), out_shape=[jax.S...  0.94 us
  transfers between devices with their start and end apart: 2, of which 1 were waited for; matrix products, arithmetic and copies ran while one was open for 0% of the time, Pallas kernels for 3%

profile of v6, /device:TPU:0, one launch (start us, length us, event | category | flops | bytes accessed | tf_op | source)
XLA Modules:
  0.0 33.4 jit_solution(2736089829493070805)
XLA Ops:
  0.0 0.0 copy-start
  0.0 0.0 copy-start.1
  0.0 2.1 %bands.1 = bf16[16,72,128]{2,1,0:T(8,128)(2,1)S(1)} custom-call(bf16[128,2048]{1,0:T(8,128)(2,1)} %fb_hbm.1, s32[16,128]{1,0:T(8,128)} %delay_hbm.1), custom_call_target="tpu_custom_call" | custom-call | tf_op jit(solution)/shard_map/bands/pallas_call | solution.py:146
  2.1 17.8 %all_to_all.10.held_ref = bf16[16,72,128]{2,1,0:T(8,128)(2,1)S(1)} all-to-all(bf16[16,72,128]{2,1,0:T(8,128)(2,1)S(1)} %bands.1), channel_id=1, replica_groups=mesh['beam'=2,'chip'=8,'core'=2] {'chip','core'}, dimensions={0} | all-to-all | bytes 589824 | tf_op jit(solution)/shard_map/all_to_all | solution.py:451
  19.9 0.0 copy-done
  19.9 1.0 %series.1 = (f32[8,272,128]{2,1,0:T(8,128)S(1)}, f32[12,128]{1,0:T(8,128)S(1)}) custom-call(bf16[16,72,128]{2,1,0:T(8,128)(2,1)S(1)} %all_to_all.10.held_ref, s32[64,1536]{1,0:T(8,128)S(1)} %bitcast.2), custom_call_target="tpu_custom_call" | custom-call | tf_op jit(solution)/shard_map/series/pallas_call | solution.py:287
  20.8 0.2 collective-permute-start
  21.0 0.0 copy-done.1
  21.0 0.9 %box.1 = (f32[6,128,128]{2,1,0:T(8,128)S(1)}, f32[6,128,128]{2,1,0:T(8,128)S(1)}) custom-call(f32[8,272,128]{2,1,0:T(8,128)S(1)} %get-tuple-element.11.series_ref, s32[12,128]{1,0:T(8,128)S(1)} %bitcast.3), custom_call_target="tpu_custom_call" | custom-call | flops 268435456 | bytes 1048576 | tf_op jit(solution)/shard_map/box/pallas_call | solution.py:359
  22.0 0.1 collective-permute-done.other_ref
  22.1 0.4 %collective-permute-start.1 = (f32[6,128,128]{2,1,0:T(8,128)S(1)}, f32[6,128,128]{2,1,0:T(8,128)S(1)}, u32[]{:S(2)}, u32[]{:S(2)}) collective-permute-start(f32[6,128,128]{2,1,0:T(8,128)S(1)} %get-tuple-element.15), channel_id=1, source_target_pairs={{0,1},{1,0},{2,3},{3,2},{4,5},{5,4},{6,7},{7,6},{8,9},{9,8},{10,11... | collective-permute-start | bytes 1179656 | tf_op jit(solution)/shard_map/ppermute | solution.py:457
  22.4 9.8 %all_to_all.11.stat_ref = f32[8,24,128]{2,1,0:T(8,128)S(1)} all-to-all(f32[8,24,128]{2,1,0:T(8,128)S(1)} %pair.1), channel_id=1, replica_groups=mesh['beam'=2,'chip'=8,'core'=2] {'chip'}, dimensions={0} | all-to-all | bytes 196608 | tf_op jit(solution)/shard_map/all_to_all | solution.py:459
  32.3 0.0 collective-permute-done.1.came_ref
  32.3 1.1 %snr.1 = f32[1536,128]{1,0:T(8,128)} custom-call(f32[6,128,128]{2,1,0:T(8,128)S(1)} %get-tuple-element.12.keep_ref, f32[6,128,128]{2,1,0:T(8,128)S(1)} %collective-permute-done.1.came_ref, f32[8,24,128]{2,1,0:T(8,128)S(1)} %all_to_all.11.stat_ref, s32[12,128]{1,0:T(8,128)S(1)} %bitcast.4), custom_call_target="tpu_custom_call" | custom-call | tf_op jit(solution)/shard_map/snr/pallas_call | solution.py:430
  (1 shorter events, 0.0 us)
Async XLA Ops:
  0.0 19.9 %copy-start = (s32[1536,64]{0,1:T(8,128)S(1)}, s32[1536,64]{0,1:T(8,128)}, u32[]{:S(2)}) copy-start(s32[1536,64]{0,1:T(8,128)} %param.6) | copy-start | bytes 1179652
  0.0 21.0 %copy-start.1 = (s32[1536]{0:T(1024)S(1)}, s32[1536]{0:T(1024)}, u32[]{:S(2)}) copy-start(s32[1536]{0:T(1024)} %param.7) | copy-start | bytes 18436
  20.8 1.2 %collective-permute-start = (f32[12,128]{1,0:T(8,128)S(1)}, f32[12,128]{1,0:T(8,128)S(1)}, u32[]{:S(2)}, u32[]{:S(2)}) collective-permute-start(f32[12,128]{1,0:T(8,128)S(1)} %get-tuple-element.13.own_ref), channel_id=1, source_target_pairs={{0,1},{1,0},{2,3},{3,2},{4,5},{5,4},{6,7},{7,6},{8,9},{9,8},{10,11... | collective-permute-start | bytes 18440 | tf_op jit(solution)/shard_map/ppermute | solution.py:454
  22.1 10.2 %collective-permute-start.1 = (f32[6,128,128]{2,1,0:T(8,128)S(1)}, f32[6,128,128]{2,1,0:T(8,128)S(1)}, u32[]{:S(2)}, u32[]{:S(2)}) collective-permute-start(f32[6,128,128]{2,1,0:T(8,128)S(1)} %get-tuple-element.15), channel_id=1, source_target_pairs={{0,1},{1,0},{2,3},{3,2},{4,5},{5,4},{6,7},{7,6},{8,9},{9,8},{10,11... | collective-permute-start | bytes 1179656 | tf_op jit(solution)/shard_map/ppermute | solution.py:457
